TPU v7x, 32 devices: a whole 2x2x4 slice. The times are simulated.
32 devices in a mesh: dp: 8 (over z, x), tensor: 4 (over y, core).
Axes of the slice: x: 2, y: 2, z: 4, core: 2. Of those that a mesh axis runs over, the one named last changes fastest.
Arguments:
- streams: bfloat16 [128, 4, 7168], P('dp', None, 'tensor'), may hold values from -12 to 12
- mix_weight: bfloat16 [24, 4, 7168], P(None, None, 'tensor'), may hold values from -0.0625 to 0.0625
- mix_bias: float32 [24], replicated, may hold values from -4 to 4
- gate_weight: bfloat16 [18432, 7168], P('dp', 'tensor'), may hold values from -0.0625 to 0.0625
- up_weight: bfloat16 [18432, 7168], P('dp', 'tensor'), may hold values from -0.0625 to 0.0625
- down_weight: bfloat16 [18432, 7168], P('dp', 'tensor'), may hold values from -0.046875 to 0.046875
Outputs:
- new_streams: bfloat16 [128, 4, 7168], P('dp', None, 'tensor')
All inputs are finite; a program needn't handle non-finite values.
Results may differ from a plain program's by a relative error of at most 0.006.
The roundings to bfloat16 on the way count: a program that leaves them out, or rounds other values in their place, can miss the bound.
Values may be sent and summed in bfloat16 or wider, within the bound.
A program may use at most 64 MiB of HBM per device.

v0:
```python
import functools
import math

import jax
import jax.numpy as jnp
from jax import lax
from jax.experimental import pallas as pl
from jax.experimental.pallas import tpu as pltpu
from jax.sharding import PartitionSpec as P

D = 7168
ITERS = 20


epsilon = 1e-06


def normalize(sweep_index, matrix):
    matrix = matrix / jnp.sum(matrix, axis=2, keepdims=True)
    return matrix / jnp.sum(matrix, axis=1, keepdims=True)


def mixing(raw_logits, squares, mix_bias, stream_count):
    scale_inv = lax.rsqrt(squares / (stream_count * D) + epsilon)
    logits = raw_logits * scale_inv[:, None] + mix_bias[None, :]
    pre_gate = jax.nn.sigmoid(logits[:, :stream_count])
    post_gate = 2.0 * jax.nn.sigmoid(logits[:, stream_count : 2 * stream_count])
    matrix = jnp.exp(logits[:, 2 * stream_count :]).reshape(-1, stream_count, stream_count)
    matrix = lax.fori_loop(0, ITERS, normalize, matrix)
    return (pre_gate, post_gate, matrix)


def contract_last(weights, rows):
    return lax.dot_general(
        weights, rows, (((1,), (1,)), ((), ())), preferred_element_type=jnp.float32
    )


def per_device(streams, mix_weight, mix_bias, gate_weight, up_weight, down_weight):
    tok_rows, stream_count, width_local = streams.shape
    logit_count = mix_weight.shape[0]
    flat_rows = streams.reshape(tok_rows, stream_count * width_local)
    flat_weight = mix_weight.reshape(logit_count, stream_count * width_local)
    raw_logits = lax.dot_general(
        flat_rows, flat_weight, (((1,), (1,)), ((), ())), preferred_element_type=jnp.float32
    )
    stream_wide = streams.astype(jnp.float32)
    squares = jnp.sum(stream_wide * stream_wide, axis=(1, 2))
    total_logits, total_squares = lax.psum((raw_logits, squares), "tensor")
    pre_gate, post_gate, res_mix = mixing(total_logits, total_squares, mix_bias, stream_count)
    mlp_input = jnp.einsum(
        "ts,tsc->tc", pre_gate, stream_wide, precision=lax.Precision.HIGHEST
    ).astype(jnp.bfloat16)
    unit_local = gate_weight.shape[0]
    block_rows = lax.all_gather(mlp_input, "dp", axis=0, tiled=True)
    gate_part = contract_last(gate_weight, block_rows)
    up_part = contract_last(up_weight, block_rows)
    both_parts = jnp.concatenate((gate_part, up_part), axis=0)
    unit_share = lax.psum_scatter(both_parts, "tensor", scatter_dimension=1, tiled=True)
    hidden_share = (jax.nn.silu(unit_share[:unit_local]) * unit_share[unit_local:]).astype(
        jnp.bfloat16
    )
    hidden = lax.all_gather(hidden_share, "tensor", axis=1, tiled=True)
    mlp_out = lax.psum_scatter(
        lax.dot_general(
            hidden, down_weight, (((0,), (0,)), ((), ())), preferred_element_type=jnp.float32
        ),
        "dp",
        scatter_dimension=0,
        tiled=True,
    )
    mixed = jnp.einsum("tij,tjc->tic", res_mix, stream_wide, precision=lax.Precision.HIGHEST)
    mixed = mixed + post_gate[:, :, None] * mlp_out[:, None, :]
    return mixed.astype(jnp.bfloat16)


MESH = pl.DeviceIdType.MESH
UNIT_CHUNK = 256
COLUMN_CHUNK = 256
PAIR = 2
GROUP = 3
D_LAG = 4
VMEM_BUDGET = 58 * 1024 * 1024


def column(values, at):
    return values[:, at : at + 1]


def sigmoid(v):
    return 1.0 / (1.0 + jnp.exp(-v))


def layer_kernel(
    plan,
    s_hbm,
    mw_hbm,
    bias_ref,
    gate_hbm,
    up_hbm,
    down_hbm,
    out_ref,
    gate_v,
    up_v,
    down_v,
    s_raw,
    mw_raw,
    s_ref,
    mw_ref,
    part,
    part_in,
    post,
    rows_all,
    mixed,
    sums,
    pair_in,
    pair_sum,
    ring_out,
    ring_in,
    hidden,
    prod,
    cross_out,
    cross_in,
    cross_sum,
    line_out,
    line_in,
    in_sem,
    w_sem,
    a_send,
    a_recv,
    bz_send,
    bz_recv,
    bx_send,
    bx_recv,
    c1_send,
    c1_recv,
    c2_send,
    c2_recv,
    c3_send,
    c3_recv,
    c4_send,
    c4_recv,
    d1_send,
    d1_recv,
    d2_send,
    d2_recv,
):
    zs, ys, tensors, chunks, nc, columns, cc, width_all = plan
    streams, tok, width = s_ref.shape
    dp = lax.axis_index("dp")
    tp = lax.axis_index("tensor")
    z, x = lax.div(dp, PAIR), lax.rem(dp, PAIR)
    y, core = lax.div(tp, PAIR), lax.rem(tp, PAIR)
    x_peer = (z * PAIR + 1 - x, tp)
    core_peer = (dp, y * PAIR + 1 - core)

    def z_at(r):
        return lax.rem(z + r + zs, zs)

    def y_at(r):
        return lax.rem(y + r + ys, ys)

    def z_peer(r):
        return (z_at(r) * PAIR + x, tp)

    def y_peer(r):
        return (dp, y_at(r) * PAIR + core)

    def t_peer(r):
        return (dp, lax.rem(tp + r, tensors))

    def send(src, dst, ssem, rsem, peer):
        return pltpu.make_async_remote_copy(
            src_ref=src, dst_ref=dst, send_sem=ssem, recv_sem=rsem, device_id=peer, device_id_type=MESH
        )

    def weight_copy(k, which):
        hbm, vmem = ((gate_hbm, gate_v), (up_hbm, up_v), (down_hbm, down_v))[which]
        return pltpu.make_async_copy(hbm.at[pl.ds(k * nc, nc)], vmem.at[pl.ds(k * nc, nc)], w_sem.at[which, k])

    def start_gate_up(k, _):
        weight_copy(k, 0).start()
        weight_copy(k, 1).start()
        return 0

    def start_down(k, _):
        weight_copy(k, 2).start()
        return 0

    barrier = pltpu.get_barrier_semaphore()
    peers = [t_peer(r) for r in range(1, tensors)] + [x_peer] + [z_peer(r) for r in range(1, zs)]
    for peer in peers:
        pl.semaphore_signal(barrier, inc=1, device_id=peer, device_id_type=MESH)

    inputs = (
        pltpu.make_async_copy(s_hbm, s_raw, in_sem.at[0]),
        pltpu.make_async_copy(mw_hbm, mw_raw, in_sem.at[1]),
    )
    for copy in inputs:
        copy.start()
    lax.fori_loop(0, chunks, start_gate_up, 0)
    lax.fori_loop(0, chunks, start_down, 0)
    for copy in inputs:
        copy.wait()
    for j in range(streams):
        s_ref[j] = s_raw[:, j, :]
        mw_ref[j] = mw_raw[:, j, :]

    raw = jnp.zeros((tok, mw_ref.shape[1]), jnp.float32)
    squares = jnp.zeros((tok, 1), jnp.float32)
    for j in range(streams):
        raw += contract_last(s_ref[j], mw_ref[j])
        wide = s_ref[j].astype(jnp.float32)
        squares += jnp.sum(wide * wide, axis=1, keepdims=True)
    count = raw.shape[1]
    part[...] = jnp.broadcast_to(squares, part.shape)
    part[:, :count] = raw
    pl.semaphore_wait(barrier, len(peers))

    def a_copy(r):
        return send(part, part_in.at[r - 1], a_send.at[r - 1], a_recv.at[r - 1], t_peer(r))

    for r in range(1, tensors):
        a_copy(r).start()
    for r in range(1, tensors):
        a_copy(r).wait_recv()
    total = part[...]
    for r in range(1, tensors):
        total = total + part_in[r - 1]
    scale_inv = lax.rsqrt(column(total, count) / width_all + epsilon)
    logits = total[:, :count] * scale_inv + bias_ref[...]
    gates = sigmoid(logits)
    mlp_input = column(gates, 0) * s_ref[0].astype(jnp.float32)
    for j in range(1, streams):
        mlp_input += column(gates, j) * s_ref[j].astype(jnp.float32)
    rows_all[z] = mlp_input.astype(jnp.bfloat16)

    def bz_copy(r):
        return send(rows_all.at[z], rows_all.at[z], bz_send.at[r - 1], bz_recv.at[r - 1], z_peer(r))

    def bx_copy(r):
        at = z_at(-r)
        return send(rows_all.at[at], rows_all.at[zs + at], bx_send.at[r], bx_recv.at[r], x_peer)

    bx_copy(0).start()
    for r in range(1, zs):
        bz_copy(r).start()
    for i in range(streams):
        post[i] = jnp.broadcast_to(2.0 * column(gates, streams + i), (tok, post.shape[2]))

    entries = jnp.exp(logits)
    mat = tuple(column(entries, 2 * streams + at) for at in range(streams * streams))

    def sweep(_, m):
        m = list(m)
        for i in range(streams):
            total_row = m[i * streams]
            for j in range(1, streams):
                total_row = total_row + m[i * streams + j]
            inv = 1.0 / total_row
            for j in range(streams):
                m[i * streams + j] = m[i * streams + j] * inv
        for j in range(streams):
            total_col = m[j]
            for i in range(1, streams):
                total_col = total_col + m[i * streams + j]
            inv = 1.0 / total_col
            for i in range(streams):
                m[i * streams + j] = m[i * streams + j] * inv
        return tuple(m)

    order = sorted(range(1, zs), key=lambda r: min(r, zs - r))
    share = ITERS // zs
    for r in order:
        mat = lax.fori_loop(0, share, sweep, mat)
        send(rows_all.at[z], rows_all.at[z_at(-r)], bz_send.at[r - 1], bz_recv.at[r - 1], z_peer(r)).wait_recv()
        bx_copy(r).start()
    mat = lax.fori_loop(0, ITERS - share * len(order), sweep, mat)
    for i in range(streams):
        line = mat[i * streams] * s_ref[0].astype(jnp.float32)
        for j in range(1, streams):
            line += mat[i * streams + j] * s_ref[j].astype(jnp.float32)
        mixed[i] = line

    def bx_arrival(r):
        at = z_at(-r)
        return send(rows_all.at[at], rows_all.at[zs + at], bx_send.at[r], bx_recv.at[r], x_peer)

    for r in range(zs):
        bx_arrival(r).wait_recv()

    prod[...] = jnp.zeros_like(prod)
    group = GROUP if chunks % GROUP == 0 else 1

    tokens = PAIR * zs * tok
    half = tokens // PAIR
    quarter = half // ys
    own_slot = core * ys + y

    def c1_copy(k):
        return send(sums.at[k, 1 - core], pair_in.at[k], c1_send.at[k], c1_recv.at[k], core_peer)

    def c2_copy(k, r):
        at = (k * (ys - 1)) + r - 1
        return send(ring_out.at[at], ring_in.at[at], c2_send.at[at], c2_recv.at[at], y_peer(r))

    def units(k):
        return pl.ds(pl.multiple_of(k * nc, nc), nc)

    def c3_copy(k, r):
        at = (k * (ys - 1)) + r - 1
        piece = hidden.at[own_slot, :, units(k)]
        return send(piece, piece, c3_send.at[at], c3_recv.at[at], y_peer(r))

    def c3_arrival(k, r):
        at = (k * (ys - 1)) + r - 1
        piece = hidden.at[core * ys + y_at(-r), :, units(k)]
        return send(piece, piece, c3_send.at[at], c3_recv.at[at], y_peer(r))

    def c4_copy(k, r):
        at = k * ys + r
        piece = hidden.at[core * ys + y_at(-r), :, units(k)]
        return send(piece, piece, c4_send.at[at], c4_recv.at[at], core_peer)

    def c4_arrival(k, r):
        at = k * ys + r
        piece = hidden.at[(1 - core) * ys + y_at(-r), :, units(k)]
        return send(piece, piece, c4_send.at[at], c4_recv.at[at], core_peer)

    def c_first(k):
        weight_copy(k, 0).wait()
        weight_copy(k, 1).wait()
        rows = rows_all[...].reshape(tokens, width)
        sums[k, :, :, :nc] = contract_last(rows, gate_v[pl.ds(k * nc, nc)]).reshape(PAIR, half, nc)
        sums[k, :, :, nc:] = contract_last(rows, up_v[pl.ds(k * nc, nc)]).reshape(PAIR, half, nc)
        c1_copy(k).start()

    def c_second(k):
        c1_copy(k).wait_recv()
        both = sums[k, core] + pair_in[k]
        pair_sum[k] = both.reshape(ys, quarter, PAIR * nc)
        for r in range(1, ys):
            ring_out[k * (ys - 1) + r - 1] = pair_sum[k, y_at(r)].astype(jnp.bfloat16)
            c2_copy(k, r).start()

    def c_third(k):
        both = pair_sum[k, y]
        for r in range(1, ys):
            c2_copy(k, r).wait_recv()
            both = both + ring_in[k * (ys - 1) + r - 1].astype(jnp.float32)
        gate, up = both[:, :nc], both[:, nc:]
        hidden[own_slot, :, units(k)] = (gate / (1.0 + jnp.exp(-gate)) * up).astype(jnp.bfloat16)
        for r in range(1, ys):
            c3_copy(k, r).start()
        c4_copy(k, 0).start()

    def c_fourth(k):
        for r in range(1, ys):
            c3_arrival(k, r).wait_recv()
            c4_copy(k, r).start()

    def pipeline(count, stages):
        last = max(lag for lag, _ in stages)

        def step(t, _):
            for lag, stage in stages:
                @pl.when(jnp.logical_and(t >= lag, t < count + lag))
                def _():
                    stage(t - lag)

            return 0

        lax.fori_loop(0, count + last, step, 0)

    def cols(n):
        return pl.ds(pl.multiple_of(n * cc, cc), cc)

    def down_piece(first, n):
        span = pl.ds(pl.multiple_of(first * nc, nc), group * nc)
        rows = hidden[:, :, span].reshape(tokens, group * nc)
        return jnp.dot(rows, down_v[span, cols(n)], preferred_element_type=jnp.float32)

    def c_fifth(k):
        for r in range(ys):
            c4_arrival(k, r).wait_recv()
        weight_copy(k, 2).wait()

        @pl.when(jnp.logical_and(lax.rem(k, group) == group - 1, k < chunks - group))
        def _():
            def add(n, _):
                prod[n] = prod[n] + down_piece(k - (group - 1), n)
                return 0

            lax.fori_loop(0, columns, add, 0)

    pipeline(chunks, ((0, c_first), (2, c_second), (5, c_third), (8, c_fourth), (10, c_fifth)))

    def d1_copy(n):
        return send(cross_out.at[n], cross_in.at[n], d1_send.at[n], d1_recv.at[n], x_peer)

    def d2_copy(n, r):
        at = n * (zs - 1) + r - 1
        return send(line_out.at[at], line_in.at[at], d2_send.at[at], d2_recv.at[at], z_peer(r))

    def d_first(n):
        product = prod[n] + down_piece(chunks - group, n)
        prod[n, :half] = product[:half]
        cross_out[n] = product[half:].astype(jnp.bfloat16)
        d1_copy(n).start()

    def d_second(n):
        d1_copy(n).wait_recv()
        cross_sum[n] = (prod[n, :half] + cross_in[n].astype(jnp.float32)).reshape(zs, tok, cc)
        for r in range(1, zs):
            line_out[n * (zs - 1) + r - 1] = cross_sum[n, z_at(r)].astype(jnp.bfloat16)
            d2_copy(n, r).start()

    def d_third(n):
        mlp_out = cross_sum[n, z]
        for r in range(1, zs):
            d2_copy(n, r).wait_recv()
            mlp_out = mlp_out + line_in[n * (zs - 1) + r - 1].astype(jnp.float32)
        for i in range(streams):
            out_ref[i, :, cols(n)] = (mixed[i, :, cols(n)] + column(post[i], 0) * mlp_out).astype(jnp.bfloat16)

    pipeline(columns, ((0, d_first), (D_LAG, d_second), (2 * D_LAG, d_third)))

    for r in range(1, tensors):
        a_copy(r).wait_send()
    for r in range(1, zs):
        bz_copy(r).wait_send()
    for r in range(zs):
        bx_copy(r).wait_send()

    def drain_c(k, _):
        c1_copy(k).wait_send()
        for r in range(1, ys):
            c2_copy(k, r).wait_send()
            c3_copy(k, r).wait_send()
        for r in range(ys):
            c4_copy(k, r).wait_send()
        return 0

    def drain_d(n, _):
        d1_copy(n).wait_send()
        for r in range(1, zs):
            d2_copy(n, r).wait_send()
        return 0

    lax.fori_loop(0, chunks, drain_c, 0)
    lax.fori_loop(0, columns, drain_d, 0)


def layer_scratch(zs, ys, tensors, tok, streams, logits, width, units, nc, cc):
    tokens = PAIR * zs * tok
    half = tokens // PAIR
    quarter = half // ys
    chunks, columns = units // nc, width // cc
    f32, bf16 = jnp.float32, jnp.bfloat16
    lanes = 128
    arrays = [
        ((units, width), bf16),
        ((units, width), bf16),
        ((units, width), bf16),
        ((tok, streams, width), bf16),
        ((logits, streams, width), bf16),
        ((streams, tok, width), bf16),
        ((streams, logits, width), bf16),
        ((tok, lanes), f32),
        ((tensors - 1, tok, lanes), f32),
        ((streams, tok, lanes), f32),
        ((PAIR * zs, tok, width), bf16),
        ((streams, tok, width), f32),
        ((chunks, PAIR, half, 2 * nc), f32),
        ((chunks, half, 2 * nc), f32),
        ((chunks, ys, quarter, 2 * nc), f32),
        ((chunks * (ys - 1), quarter, 2 * nc), bf16),
        ((chunks * (ys - 1), quarter, 2 * nc), bf16),
        ((PAIR * ys, quarter, units), bf16),
        ((columns, tokens, cc), f32),
        ((columns, half, cc), bf16),
        ((columns, half, cc), bf16),
        ((columns, zs, tok, cc), f32),
        ((columns * (zs - 1), tok, cc), bf16),
        ((columns * (zs - 1), tok, cc), bf16),
    ]
    both = lambda count: [(count,), (count,)]
    sems = [(2,), (3, chunks)]
    for count in (tensors - 1, zs - 1, zs, chunks, chunks * (ys - 1), chunks * (ys - 1), chunks * ys, columns, columns * (zs - 1)):
        sems += both(count)
    size = sum(math.prod(shape) * jnp.dtype(kind).itemsize for shape, kind in arrays)
    return arrays, sems, size


def fused(mesh, streams, mix_weight, mix_bias, gate_weight, up_weight, down_weight):
    tok, stream_count, width = streams.shape
    units = gate_weight.shape[0]
    dps, tensors = mesh.shape["dp"], mesh.shape["tensor"]
    zs, ys = dps // PAIR, tensors // PAIR
    nc, cc = UNIT_CHUNK, COLUMN_CHUNK
    arrays, sems, _ = layer_scratch(zs, ys, tensors, tok, stream_count, mix_weight.shape[0], width, units, nc, cc)
    plan = (zs, ys, tensors, units // nc, nc, width // cc, cc, stream_count * width * tensors)
    bias = mix_bias[None, :]
    vmem = pl.BlockSpec(memory_space=pltpu.VMEM)
    hbm = pl.BlockSpec(memory_space=pl.ANY)
    out = pl.pallas_call(
        functools.partial(layer_kernel, plan),
        out_shape=jax.ShapeDtypeStruct((stream_count, tok, width), jnp.bfloat16),
        in_specs=[hbm, hbm, vmem, hbm, hbm, hbm],
        out_specs=vmem,
        scratch_shapes=[pltpu.VMEM(shape, kind) for shape, kind in arrays]
        + [pltpu.SemaphoreType.DMA(shape) for shape in sems],
        compiler_params=pltpu.CompilerParams(
            collective_id=0, has_side_effects=True, vmem_limit_bytes=VMEM_BUDGET
        ),
    )(streams, mix_weight, bias, gate_weight, up_weight, down_weight)
    return out.transpose(1, 0, 2)


def fits(mesh, streams, mix_weight, gate_weight):
    tok, stream_count, width = streams.shape
    units = gate_weight.shape[0]
    dps, tensors = mesh.shape["dp"], mesh.shape["tensor"]
    if dps % PAIR or tensors % PAIR or dps < 2 * PAIR or tensors < 2 * PAIR:
        return False
    zs, ys = dps // PAIR, tensors // PAIR
    if units % UNIT_CHUNK or width % COLUMN_CHUNK or tok % 16 or (zs * tok) % (16 * ys):
        return False
    if mix_weight.shape[0] >= 128:
        return False
    size = layer_scratch(
        zs, ys, tensors, tok, stream_count, mix_weight.shape[0], width, units, UNIT_CHUNK, COLUMN_CHUNK
    )[2]
    return size < VMEM_BUDGET * 3 // 4


def solution(mesh):
    in_specs = (
        P("dp", None, "tensor"),
        P(None, None, "tensor"),
        P(),
        P("dp", "tensor"),
        P("dp", "tensor"),
        P("dp", "tensor"),
    )
    out_specs = P("dp", None, "tensor")

    def step(streams, mix_weight, mix_bias, gate_weight, up_weight, down_weight):
        operands = (streams, mix_weight, mix_bias, gate_weight, up_weight, down_weight)
        if fits(mesh, streams, mix_weight, gate_weight):
            return fused(mesh, *operands)
        return per_device(*operands)

    return jax.shard_map(step, mesh=mesh, in_specs=in_specs, out_specs=out_specs, check_vma=False)
```

profile of v0, /device:TPU:0, one launch (start us, length us, event | category | flops | bytes accessed | tf_op | source)
XLA Modules:
  0.0 54.7 jit_solution(9407851145564147960)
XLA Ops:
  0.0 52.9 %shard_map.64 = bf16[4,16,1792]{2,1,0:T(8,128)(2,1)} custom-call(bf16[16,4,1792]{2,1,0:T(4,128)(2,1)} %s_hbm.1, bf16[24,4,1792]{2,1,0:T(4,128)(2,1)} %mw_hbm.1, f32[1,24]{1,0:T(1,128)} %bitcast.3, bf16[2304,1792]{1,0:T(8,128)(2,1)} %gate_hbm.1, bf16[2304,1792]{1,0:T(8,128)(2,1)} %up_hbm.1, bf16[2304,1792]{1,0:T(8,128)(2,1)} %down_hbm.1), custom_call_target="tpu_custom_call" | custom-call | tf_op jit(solution)/shard_map/pallas_call | solution.py:506
  52.9 1.7 %copy.7 = bf16[16,4,1792]{2,1,0:T(4,128)(2,1)} copy(bf16[16,4,1792]{2,0,1:T(8,128)(2,1)} %bitcast.2) | data formatting | bytes 458752 | tf_op jit(solution)/shard_map/transpose | solution.py:517
where the time goes:
time: 54.8 us; the launch traced here: 54.7 us
  Pallas kernels  52.9 us (97%)
  local copies, waits for them, and re-layouts  1.75 us (3%)
    pallas_call x1, Pallas kernels, fused(): pl.pallas_call(functools.partial(layer_kernel, plan), out_shape=jax.Shape...  52.9 us
    transpose x1, local copies, waits for them, and re-layouts, fused(): return out.transpose(1, 0, 2)  1.75 us

commit v1 on v0

--- a/solution.py
+++ b/solution.py
@@ -99,6 +99,7 @@
     gate_hbm,
     up_hbm,
     down_hbm,
+    out_hbm,
     out_ref,
     gate_v,
     up_v,
@@ -124,6 +125,7 @@
     cross_sum,
     line_out,
     line_in,
+    entry,
     in_sem,
     w_sem,
     a_send,
@@ -144,6 +146,7 @@
     d1_recv,
     d2_send,
     d2_recv,
+    out_sem,
 ):
     zs, ys, tensors, chunks, nc, columns, cc, width_all = plan
     streams, tok, width = s_ref.shape
@@ -176,7 +179,11 @@
 
     def weight_copy(k, which):
         hbm, vmem = ((gate_hbm, gate_v), (up_hbm, up_v), (down_hbm, down_v))[which]
-        return pltpu.make_async_copy(hbm.at[pl.ds(k * nc, nc)], vmem.at[pl.ds(k * nc, nc)], w_sem.at[which, k])
+        return pltpu.make_async_copy(hbm.at[pl.ds(k * nc, nc)], vmem.at[pl.ds(k * nc, nc)], w_sem.at[which])
+
+    def weight_wait(which):
+        hbm, vmem = ((gate_hbm, gate_v), (up_hbm, up_v), (down_hbm, down_v))[which]
+        pltpu.make_async_copy(hbm, vmem, w_sem.at[which]).wait()
 
     def start_gate_up(k, _):
         weight_copy(k, 0).start()
@@ -218,12 +225,14 @@
     pl.semaphore_wait(barrier, len(peers))
 
     def a_copy(r):
-        return send(part, part_in.at[r - 1], a_send.at[r - 1], a_recv.at[r - 1], t_peer(r))
+        return send(part, part_in.at[r - 1], a_send.at[0], a_recv.at[0], t_peer(r))
+
+    def a_all():
+        return send(part_in, part_in, a_send.at[0], a_recv.at[0], t_peer(1))
 
     for r in range(1, tensors):
         a_copy(r).start()
-    for r in range(1, tensors):
-        a_copy(r).wait_recv()
+    a_all().wait_recv()
     total = part[...]
     for r in range(1, tensors):
         total = total + part_in[r - 1]
@@ -236,11 +245,11 @@
     rows_all[z] = mlp_input.astype(jnp.bfloat16)
 
     def bz_copy(r):
-        return send(rows_all.at[z], rows_all.at[z], bz_send.at[r - 1], bz_recv.at[r - 1], z_peer(r))
+        return send(rows_all.at[z], rows_all.at[z], bz_send.at[0], bz_recv.at[r - 1], z_peer(r))
 
     def bx_copy(r):
         at = z_at(-r)
-        return send(rows_all.at[at], rows_all.at[zs + at], bx_send.at[r], bx_recv.at[r], x_peer)
+        return send(rows_all.at[at], rows_all.at[zs + at], bx_send.at[0], bx_recv.at[0], x_peer)
 
     bx_copy(0).start()
     for r in range(1, zs):
@@ -248,8 +257,15 @@
     for i in range(streams):
         post[i] = jnp.broadcast_to(2.0 * column(gates, streams + i), (tok, post.shape[2]))
 
-    entries = jnp.exp(logits)
-    mat = tuple(column(entries, 2 * streams + at) for at in range(streams * streams))
+    order = sorted(range(1, zs), key=lambda r: min(r, zs - r))
+    for r in order:
+        send(rows_all.at[z], rows_all.at[z_at(-r)], bz_send.at[0], bz_recv.at[r - 1], z_peer(r)).wait_recv()
+        bx_copy(r).start()
+
+    entry[...] = jnp.zeros_like(entry)
+    entry[:, :count] = jnp.exp(logits)
+    turned = entry[...].T
+    mat = tuple(turned[2 * streams + at : 2 * streams + at + 1] for at in range(streams * streams))
 
     def sweep(_, m):
         m = list(m)
@@ -269,25 +285,22 @@
                 m[i * streams + j] = m[i * streams + j] * inv
         return tuple(m)
 
-    order = sorted(range(1, zs), key=lambda r: min(r, zs - r))
-    share = ITERS // zs
-    for r in order:
-        mat = lax.fori_loop(0, share, sweep, mat)
-        send(rows_all.at[z], rows_all.at[z_at(-r)], bz_send.at[r - 1], bz_recv.at[r - 1], z_peer(r)).wait_recv()
-        bx_copy(r).start()
-    mat = lax.fori_loop(0, ITERS - share * len(order), sweep, mat)
+    mat = lax.fori_loop(0, ITERS, sweep, mat)
+    res = jnp.concatenate(mat + (jnp.zeros((128 - len(mat), tok), jnp.float32),), axis=0).T
     for i in range(streams):
-        line = mat[i * streams] * s_ref[0].astype(jnp.float32)
+        line = column(res, i * streams) * s_ref[0].astype(jnp.float32)
         for j in range(1, streams):
-            line += mat[i * streams + j] * s_ref[j].astype(jnp.float32)
+            line += column(res, i * streams + j) * s_ref[j].astype(jnp.float32)
         mixed[i] = line
 
-    def bx_arrival(r):
-        at = z_at(-r)
-        return send(rows_all.at[at], rows_all.at[zs + at], bx_send.at[r], bx_recv.at[r], x_peer)
-
-    for r in range(zs):
-        bx_arrival(r).wait_recv()
+    received = rows_all.at[pl.ds(zs, zs)]
+
+    def bx_all():
+        return send(received, received, bx_send.at[0], bx_recv.at[0], x_peer)
+
+    bx_all().wait_recv()
+    for which in range(3):
+        weight_wait(which)
 
     prod[...] = jnp.zeros_like(prod)
     group = GROUP if chunks % GROUP == 0 else 1
@@ -298,11 +311,11 @@
     own_slot = core * ys + y
 
     def c1_copy(k):
-        return send(sums.at[k, 1 - core], pair_in.at[k], c1_send.at[k], c1_recv.at[k], core_peer)
+        return send(sums.at[k, 1 - core], pair_in.at[k], c1_send.at[0], c1_recv.at[k], core_peer)
 
     def c2_copy(k, r):
         at = (k * (ys - 1)) + r - 1
-        return send(ring_out.at[at], ring_in.at[at], c2_send.at[at], c2_recv.at[at], y_peer(r))
+        return send(ring_out.at[at], ring_in.at[at], c2_send.at[0], c2_recv.at[at], y_peer(r))
 
     def units(k):
         return pl.ds(pl.multiple_of(k * nc, nc), nc)
@@ -310,26 +323,22 @@
     def c3_copy(k, r):
         at = (k * (ys - 1)) + r - 1
         piece = hidden.at[own_slot, :, units(k)]
-        return send(piece, piece, c3_send.at[at], c3_recv.at[at], y_peer(r))
+        return send(piece, piece, c3_send.at[0], c3_recv.at[at], y_peer(r))
 
     def c3_arrival(k, r):
         at = (k * (ys - 1)) + r - 1
         piece = hidden.at[core * ys + y_at(-r), :, units(k)]
-        return send(piece, piece, c3_send.at[at], c3_recv.at[at], y_peer(r))
+        return send(piece, piece, c3_send.at[0], c3_recv.at[at], y_peer(r))
 
     def c4_copy(k, r):
-        at = k * ys + r
         piece = hidden.at[core * ys + y_at(-r), :, units(k)]
-        return send(piece, piece, c4_send.at[at], c4_recv.at[at], core_peer)
-
-    def c4_arrival(k, r):
-        at = k * ys + r
-        piece = hidden.at[(1 - core) * ys + y_at(-r), :, units(k)]
-        return send(piece, piece, c4_send.at[at], c4_recv.at[at], core_peer)
+        return send(piece, piece, c4_send.at[0], c4_recv.at[k], core_peer)
+
+    def c4_arrival(k):
+        piece = hidden.at[pl.ds((1 - core) * ys, ys), :, units(k)]
+        return send(piece, piece, c4_send.at[0], c4_recv.at[k], core_peer)
 
     def c_first(k):
-        weight_copy(k, 0).wait()
-        weight_copy(k, 1).wait()
         rows = rows_all[...].reshape(tokens, width)
         sums[k, :, :, :nc] = contract_last(rows, gate_v[pl.ds(k * nc, nc)]).reshape(PAIR, half, nc)
         sums[k, :, :, nc:] = contract_last(rows, up_v[pl.ds(k * nc, nc)]).reshape(PAIR, half, nc)
@@ -381,9 +390,7 @@
         return jnp.dot(rows, down_v[span, cols(n)], preferred_element_type=jnp.float32)
 
     def c_fifth(k):
-        for r in range(ys):
-            c4_arrival(k, r).wait_recv()
-        weight_copy(k, 2).wait()
+        c4_arrival(k).wait_recv()
 
         @pl.when(jnp.logical_and(lax.rem(k, group) == group - 1, k < chunks - group))
         def _():
@@ -396,11 +403,15 @@
     pipeline(chunks, ((0, c_first), (2, c_second), (5, c_third), (8, c_fourth), (10, c_fifth)))
 
     def d1_copy(n):
-        return send(cross_out.at[n], cross_in.at[n], d1_send.at[n], d1_recv.at[n], x_peer)
+        return send(cross_out.at[n], cross_in.at[n], d1_send.at[0], d1_recv.at[n], x_peer)
 
     def d2_copy(n, r):
         at = n * (zs - 1) + r - 1
-        return send(line_out.at[at], line_in.at[at], d2_send.at[at], d2_recv.at[at], z_peer(r))
+        return send(line_out.at[at], line_in.at[at], d2_send.at[0], d2_recv.at[n], z_peer(r))
+
+    def d2_arrival(n):
+        piece = line_in.at[pl.ds(n * (zs - 1), zs - 1)]
+        return send(piece, piece, d2_send.at[0], d2_recv.at[n], z_peer(1))
 
     def d_first(n):
         product = prod[n] + down_piece(chunks - group, n)
@@ -417,38 +428,32 @@
 
     def d_third(n):
         mlp_out = cross_sum[n, z]
+        d2_arrival(n).wait_recv()
         for r in range(1, zs):
-            d2_copy(n, r).wait_recv()
             mlp_out = mlp_out + line_in[n * (zs - 1) + r - 1].astype(jnp.float32)
         for i in range(streams):
             out_ref[i, :, cols(n)] = (mixed[i, :, cols(n)] + column(post[i], 0) * mlp_out).astype(jnp.bfloat16)
+        pltpu.make_async_copy(out_ref.at[:, :, cols(n)], out_hbm.at[:, :, cols(n)], out_sem.at[0]).start()
 
     pipeline(columns, ((0, d_first), (D_LAG, d_second), (2 * D_LAG, d_third)))
 
-    for r in range(1, tensors):
-        a_copy(r).wait_send()
-    for r in range(1, zs):
-        bz_copy(r).wait_send()
-    for r in range(zs):
-        bx_copy(r).wait_send()
-
-    def drain_c(k, _):
-        c1_copy(k).wait_send()
-        for r in range(1, ys):
-            c2_copy(k, r).wait_send()
-            c3_copy(k, r).wait_send()
-        for r in range(ys):
-            c4_copy(k, r).wait_send()
-        return 0
-
-    def drain_d(n, _):
-        d1_copy(n).wait_send()
-        for r in range(1, zs):
-            d2_copy(n, r).wait_send()
-        return 0
-
-    lax.fori_loop(0, chunks, drain_c, 0)
-    lax.fori_loop(0, columns, drain_d, 0)
+    a_all().wait_send()
+    sent = rows_all.at[pl.ds(0, zs - 1)]
+    send(sent, sent, bz_send.at[0], bz_recv.at[0], z_peer(1)).wait_send()
+    bx_all().wait_send()
+    whole = [
+        (pair_in, c1_send),
+        (ring_in, c2_send),
+        (cross_in, d1_send),
+        (line_in, d2_send),
+    ]
+    for ref, sem in whole:
+        send(ref, ref, sem.at[0], sem.at[0], x_peer).wait_send()
+    own = hidden.at[pl.ds(0, ys - 1)]
+    send(own, own, c3_send.at[0], c3_send.at[0], x_peer).wait_send()
+    both = hidden.at[pl.ds(0, ys)]
+    send(both, both, c4_send.at[0], c4_send.at[0], x_peer).wait_send()
+    pltpu.make_async_copy(out_ref, out_hbm, out_sem.at[0]).wait()
 
 
 def layer_scratch(zs, ys, tensors, tok, streams, logits, width, units, nc, cc):
@@ -459,6 +464,7 @@
     f32, bf16 = jnp.float32, jnp.bfloat16
     lanes = 128
     arrays = [
+        ((streams, tok, width), bf16),
         ((units, width), bf16),
         ((units, width), bf16),
         ((units, width), bf16),
@@ -483,11 +489,12 @@
         ((columns, zs, tok, cc), f32),
         ((columns * (zs - 1), tok, cc), bf16),
         ((columns * (zs - 1), tok, cc), bf16),
+        ((tok, lanes), f32),
     ]
-    both = lambda count: [(count,), (count,)]
-    sems = [(2,), (3, chunks)]
-    for count in (tensors - 1, zs - 1, zs, chunks, chunks * (ys - 1), chunks * (ys - 1), chunks * ys, columns, columns * (zs - 1)):
-        sems += both(count)
+    sems = [(2,), (3,)]
+    for count in (1, zs - 1, 1, chunks, chunks * (ys - 1), chunks * (ys - 1), chunks, columns, columns):
+        sems += [(1,), (count,)]
+    sems.append((1,))
     size = sum(math.prod(shape) * jnp.dtype(kind).itemsize for shape, kind in arrays)
     return arrays, sems, size
 
@@ -507,7 +514,7 @@
         functools.partial(layer_kernel, plan),
         out_shape=jax.ShapeDtypeStruct((stream_count, tok, width), jnp.bfloat16),
         in_specs=[hbm, hbm, vmem, hbm, hbm, hbm],
-        out_specs=vmem,
+        out_specs=hbm,
         scratch_shapes=[pltpu.VMEM(shape, kind) for shape, kind in arrays]
         + [pltpu.SemaphoreType.DMA(shape) for shape in sems],
         compiler_params=pltpu.CompilerParams(

time: 54.8 us -> 52.1 us (0.951)
  Pallas kernels: 52.9 us -> 50.2 us
    pallas_call x1, Pallas kernels: 52.9 us -> 50.2 us  [fused(): pl.pallas_call(functools.partial(layer_kernel, plan), out_shape=jax.Shape...]
where the time goes in v1:
time: 52.1 us; the launch traced here: 51.9 us
  Pallas kernels  50.2 us (96%)
  local copies, waits for them, and re-layouts  1.75 us (3%)
    pallas_call x1, Pallas kernels, fused(): pl.pallas_call(functools.partial(layer_kernel, plan), out_shape=jax.Shape...  50.2 us
    transpose x1, local copies, waits for them, and re-layouts, fused(): return out.transpose(1, 0, 2)  1.75 us

profile of v1, /device:TPU:0, one launch (start us, length us, event | category | flops | bytes accessed | tf_op | source)
XLA Modules:
  0.0 51.9 jit_solution(9818819515739884449)
XLA Ops:
  0.0 50.2 %shard_map.64 = bf16[4,16,1792]{2,1,0:T(8,128)(2,1)} custom-call(bf16[16,4,1792]{2,1,0:T(4,128)(2,1)} %s_hbm.1, bf16[24,4,1792]{2,1,0:T(4,128)(2,1)} %mw_hbm.1, f32[1,24]{1,0:T(1,128)} %bitcast.3, bf16[2304,1792]{1,0:T(8,128)(2,1)} %gate_hbm.1, bf16[2304,1792]{1,0:T(8,128)(2,1)} %up_hbm.1, bf16[2304,1792]{1,0:T(8,128)(2,1)} %down_hbm.1), custom_call_target="tpu_custom_call" | custom-call | tf_op jit(solution)/shard_map/pallas_call | solution.py:513
  50.2 1.7 %copy.7 = bf16[16,4,1792]{2,1,0:T(4,128)(2,1)} copy(bf16[16,4,1792]{2,0,1:T(8,128)(2,1)} %bitcast.2) | data formatting | bytes 458752 | tf_op jit(solution)/shard_map/transpose | solution.py:524

commit v2 on v1

v2 whole, which is shorter than its diff:
```python
import functools
import math

import jax
import jax.numpy as jnp
from jax import lax
from jax.experimental import pallas as pl
from jax.experimental.pallas import tpu as pltpu
from jax.sharding import PartitionSpec as P

D = 7168
ITERS = 20


epsilon = 1e-06


def normalize(sweep_index, matrix):
    matrix = matrix / jnp.sum(matrix, axis=2, keepdims=True)
    return matrix / jnp.sum(matrix, axis=1, keepdims=True)


def mixing(raw_logits, squares, mix_bias, stream_count):
    scale_inv = lax.rsqrt(squares / (stream_count * D) + epsilon)
    logits = raw_logits * scale_inv[:, None] + mix_bias[None, :]
    pre_gate = jax.nn.sigmoid(logits[:, :stream_count])
    post_gate = 2.0 * jax.nn.sigmoid(logits[:, stream_count : 2 * stream_count])
    matrix = jnp.exp(logits[:, 2 * stream_count :]).reshape(-1, stream_count, stream_count)
    matrix = lax.fori_loop(0, ITERS, normalize, matrix)
    return (pre_gate, post_gate, matrix)


def contract_last(weights, rows):
    return lax.dot_general(
        weights, rows, (((1,), (1,)), ((), ())), preferred_element_type=jnp.float32
    )


def per_device(streams, mix_weight, mix_bias, gate_weight, up_weight, down_weight):
    tok_rows, stream_count, width_local = streams.shape
    logit_count = mix_weight.shape[0]
    flat_rows = streams.reshape(tok_rows, stream_count * width_local)
    flat_weight = mix_weight.reshape(logit_count, stream_count * width_local)
    raw_logits = lax.dot_general(
        flat_rows, flat_weight, (((1,), (1,)), ((), ())), preferred_element_type=jnp.float32
    )
    stream_wide = streams.astype(jnp.float32)
    squares = jnp.sum(stream_wide * stream_wide, axis=(1, 2))
    total_logits, total_squares = lax.psum((raw_logits, squares), "tensor")
    pre_gate, post_gate, res_mix = mixing(total_logits, total_squares, mix_bias, stream_count)
    mlp_input = jnp.einsum(
        "ts,tsc->tc", pre_gate, stream_wide, precision=lax.Precision.HIGHEST
    ).astype(jnp.bfloat16)
    unit_local = gate_weight.shape[0]
    block_rows = lax.all_gather(mlp_input, "dp", axis=0, tiled=True)
    gate_part = contract_last(gate_weight, block_rows)
    up_part = contract_last(up_weight, block_rows)
    both_parts = jnp.concatenate((gate_part, up_part), axis=0)
    unit_share = lax.psum_scatter(both_parts, "tensor", scatter_dimension=1, tiled=True)
    hidden_share = (jax.nn.silu(unit_share[:unit_local]) * unit_share[unit_local:]).astype(
        jnp.bfloat16
    )
    hidden = lax.all_gather(hidden_share, "tensor", axis=1, tiled=True)
    mlp_out = lax.psum_scatter(
        lax.dot_general(
            hidden, down_weight, (((0,), (0,)), ((), ())), preferred_element_type=jnp.float32
        ),
        "dp",
        scatter_dimension=0,
        tiled=True,
    )
    mixed = jnp.einsum("tij,tjc->tic", res_mix, stream_wide, precision=lax.Precision.HIGHEST)
    mixed = mixed + post_gate[:, :, None] * mlp_out[:, None, :]
    return mixed.astype(jnp.bfloat16)


MESH = pl.DeviceIdType.MESH
UNIT_CHUNK = 256
COLUMN_CHUNK = 256
PAIR = 2
GROUPS = 2
LANES = 128
LAG_SUM = (3, 4)
LAG_HIDDEN = (8, 12)
LAG_FORWARD = 14
LATE = 4
LAG_CROSS = 7
LAG_OUT = 21
TURNS = (6, 4, 4)
VMEM_BUDGET = 58 * 1024 * 1024


def column(values, at):
    return values[:, at : at + 1]


def sigmoid(v):
    return 1.0 / (1.0 + jnp.exp(-v))


def sweep(count, _, entries):
    m = list(entries)
    for i in range(count):
        total_row = m[i * count]
        for j in range(1, count):
            total_row = total_row + m[i * count + j]
        inv = 1.0 / total_row
        for j in range(count):
            m[i * count + j] = m[i * count + j] * inv
    for j in range(count):
        total_col = m[j]
        for i in range(1, count):
            total_col = total_col + m[i * count + j]
        inv = 1.0 / total_col
        for i in range(count):
            m[i * count + j] = m[i * count + j] * inv
    return tuple(m)


def layer_kernel(
    plan,
    s_hbm,
    mw_hbm,
    bias_ref,
    gate_hbm,
    up_hbm,
    down_hbm,
    out_hbm,
    out_ref,
    gate_v,
    up_v,
    down_v,
    s_raw,
    mw_raw,
    s_ref,
    mw_ref,
    part,
    part_in,
    entry,
    post,
    rows_all,
    mixed,
    sums,
    pair_in,
    ring_out,
    ring_in,
    hidden,
    own,
    cross_out,
    cross_in,
    cross_sum,
    line_out,
    line_in,
    in_sem,
    w_sem,
    out_sem,
    a_send,
    a_recv,
    bz_send,
    bz_recv,
    bx_send,
    bx_recv,
    c1_send,
    c1_recv,
    c2_send,
    c2_recv,
    c3_send,
    c3_recv,
    c4_send,
    c4_recv,
    d1_send,
    d1_recv,
    d2_send,
    d2_recv,
):
    zs, ys, tensors, chunks, nc, columns, cc, width_all = plan
    streams, tok, width = s_ref.shape
    scope = jax.named_scope
    dp = lax.axis_index("dp")
    tp = lax.axis_index("tensor")
    z, x = lax.div(dp, PAIR), lax.rem(dp, PAIR)
    y, core = lax.div(tp, PAIR), lax.rem(tp, PAIR)
    x_peer = (z * PAIR + 1 - x, tp)
    core_peer = (dp, y * PAIR + 1 - core)
    zb = zs // GROUPS
    gh = zb * tok
    gq = gh // ys
    z_half, z_odd = lax.div(z, zb), lax.rem(z, zb)
    own_group = lax.rem(lax.div(z + 1, zb), GROUPS)

    def slot_of(at):
        return lax.rem(lax.div(at + 1, zb), GROUPS) * zb + lax.div(at, zb)

    def y_at(r):
        return lax.rem(y + r + ys, ys)

    def z_dev(at):
        return (at * PAIR + x, tp)

    def z_peer(r):
        return z_dev(lax.rem(z + r + zs, zs))

    def y_peer(r):
        return (dp, y_at(r) * PAIR + core)

    def t_peer(r):
        return (dp, lax.rem(tp + r, tensors))

    def send(src, dst, ssem, rsem, peer):
        return pltpu.make_async_remote_copy(
            src_ref=src, dst_ref=dst, send_sem=ssem, recv_sem=rsem, device_id=peer, device_id_type=MESH
        )

    weights = ((gate_hbm, gate_v), (up_hbm, up_v), (down_hbm, down_v))

    def start_weights(k, _, which):
        hbm, vmem = weights[which]
        part_of = pl.ds(k * nc, nc)
        pltpu.make_async_copy(hbm.at[part_of], vmem.at[part_of], w_sem.at[which]).start()
        return 0

    def weight_wait(which):
        hbm, vmem = weights[which]
        pltpu.make_async_copy(hbm, vmem, w_sem.at[which]).wait()

    barrier = pltpu.get_barrier_semaphore()
    peers = [t_peer(r) for r in range(1, tensors)] + [x_peer] + [z_peer(r) for r in range(1, zs)]
    with scope("start"):
        for peer in peers:
            pl.semaphore_signal(barrier, inc=1, device_id=peer, device_id_type=MESH)
        inputs = (
            pltpu.make_async_copy(s_hbm, s_raw, in_sem.at[0]),
            pltpu.make_async_copy(mw_hbm, mw_raw, in_sem.at[1]),
        )
        for copy in inputs:
            copy.start()
        for which in range(3):
            lax.fori_loop(0, chunks, functools.partial(start_weights, which=which), 0)
        for copy in inputs:
            copy.wait()
    with scope("relayout"):
        for j in range(streams):
            s_ref[j] = s_raw[:, j, :]
            mw_ref[j] = mw_raw[:, j, :]

    with scope("raw_logits"):
        raw = jnp.zeros((tok, mw_ref.shape[1]), jnp.float32)
        squares = jnp.zeros((tok, 1), jnp.float32)
        for j in range(streams):
            raw += contract_last(s_ref[j], mw_ref[j])
            wide = s_ref[j].astype(jnp.float32)
            squares += jnp.sum(wide * wide, axis=1, keepdims=True)
        count = raw.shape[1]
        part[...] = jnp.broadcast_to(squares, part.shape)
        part[:, :count] = raw
    with scope("barrier"):
        pl.semaphore_wait(barrier, len(peers))

    def a_copy(r):
        return send(part, part_in.at[r - 1], a_send.at[0], a_recv.at[0], t_peer(r))

    def a_all():
        return send(part_in, part_in, a_send.at[0], a_recv.at[0], t_peer(1))

    with scope("a_exchange"):
        for r in range(1, tensors):
            a_copy(r).start()
        a_all().wait_recv()
    with scope("gates"):
        total = part[...]
        for r in range(1, tensors):
            total = total + part_in[r - 1]
        scale_inv = lax.rsqrt(column(total, count) / width_all + epsilon)
        logits = total[:, :count] * scale_inv + bias_ref[...]
        gates = sigmoid(logits)
        mlp_input = column(gates, 0) * s_ref[0].astype(jnp.float32)
        for j in range(1, streams):
            mlp_input += column(gates, j) * s_ref[j].astype(jnp.float32)
        rows_all[slot_of(z)] = mlp_input.astype(jnp.bfloat16)

    mate, inner, outer = z_half * zb + 1 - z_odd, zb - z_half, (zs - 1) * (1 - z_half)

    def bz_copy(source, target):
        block = rows_all.at[slot_of(source)]
        return send(block, block, bz_send.at[0], bz_recv.at[source], z_dev(target))

    def bx_copy(source):
        at = slot_of(source)
        return send(rows_all.at[at], rows_all.at[zs + at], bx_send.at[0], bx_recv.at[0], x_peer)

    def bx_all():
        received = rows_all.at[pl.ds(zs, zs)]
        return send(received, received, bx_send.at[0], bx_recv.at[0], x_peer)

    with scope("b_start"):
        for target in (mate, outer, inner):
            bz_copy(z, target).start()
        bx_copy(z).start()
        for i in range(streams):
            post[i] = jnp.broadcast_to(2.0 * column(gates, streams + i), (tok, post.shape[2]))
    def turn(k, _, which):
        with scope("turn"):
            vmem = weights[which][1]
            span = pl.ds(pl.multiple_of(k * nc, nc), nc)
            for at in range(0, width, nc):
                vmem[span, at : at + nc] = vmem[span, at : at + nc].T
        return 0

    def turns(first, last):
        for which in range(2):
            low, high = (min(max(at - which * chunks, 0), chunks) for at in (first, last))
            if low < high:
                lax.fori_loop(low, high, functools.partial(turn, which=which), 0)

    weight_wait(0)
    turned = 0
    for at, source in enumerate((mate, inner, outer)):
        if at == 1:
            weight_wait(1)
        turns(turned, turned + TURNS[at])
        turned += TURNS[at]
        with scope(f"b_forward{at}"):
            bz_copy(source, source).wait_recv()
            bx_copy(source).start()
    turns(turned, 2 * chunks)

    with scope("sinkhorn"):
        entry[...] = jnp.zeros_like(entry)
        entry[:, :count] = jnp.exp(logits)
        flipped = entry[...].T
        first = 2 * streams
        mat = tuple(flipped[first + at : first + at + 1] for at in range(streams * streams))
        mat = lax.fori_loop(0, ITERS, functools.partial(sweep, streams), mat)
    with scope("mixed"):
        rest = jnp.zeros((LANES - len(mat), tok), jnp.float32)
        res = jnp.concatenate(mat + (rest,), axis=0).T
        for i in range(streams):
            line = column(res, i * streams) * s_ref[0].astype(jnp.float32)
            for j in range(1, streams):
                line += column(res, i * streams + j) * s_ref[j].astype(jnp.float32)
            mixed[i] = line
    with scope("b_wait"):
        bx_all().wait_recv()
        weight_wait(2)

    own_slot = core * ys + y

    def c1_copy(k):
        return send(sums.at[k, 1 - core], pair_in.at[k], c1_send.at[0], c1_recv.at[k], core_peer)

    def c2_copy(k, g, r):
        at = k * GROUPS + g
        return send(ring_out.at[at, r - 1], ring_in.at[at, r - 1], c2_send.at[0], c2_recv.at[at], y_peer(r))

    def c2_arrival(k, g):
        piece = ring_in.at[k * GROUPS + g]
        return send(piece, piece, c2_send.at[0], c2_recv.at[k * GROUPS + g], y_peer(1))

    def units(k):
        return pl.ds(pl.multiple_of(k * nc, nc), nc)

    def quarter(at):
        return pl.ds(pl.multiple_of(at * gq, gq), gq)

    def c3_copy(k, g, r, source):
        at = (k * GROUPS + g) * (ys - 1) + r - 1
        piece = hidden.at[g, core * ys + source, :, units(k)]
        return send(piece, piece, c3_send.at[0], c3_recv.at[at], y_peer(r))

    def c4_copy(k, g, source):
        piece = hidden.at[g, core * ys + source, :, units(k)]
        return send(piece, piece, c4_send.at[0], c4_recv.at[g], core_peer)

    def c4_arrival(g):
        piece = hidden.at[g, pl.ds((1 - core) * ys, ys)]
        return send(piece, piece, c4_send.at[0], c4_recv.at[g], core_peer)

    def c_first(k):
        with scope("c_first"):
            rows = rows_all[...].reshape(PAIR * zs * tok, width)
            shape = (PAIR, GROUPS, gh, nc)
            for at, vmem in ((pl.ds(0, nc), gate_v), (pl.ds(nc, nc), up_v)):
                product = None
                for kt in range(0, width, nc):
                    term = jnp.dot(rows[:, kt : kt + nc], vmem[pl.ds(k * nc, nc), kt : kt + nc], preferred_element_type=jnp.float32)
                    product = term if product is None else product + term
                sums[k, :, :, :, at] = product.reshape(shape)
            c1_copy(k).start()

    def c_second(g, k):
        with scope(f"c_second{g}"):
            if g == 0:
                c1_copy(k).wait_recv()
            for r in range(1, ys):
                at = quarter(y_at(r))
                both = sums[k, core, g, at] + pair_in[k, g, at]
                ring_out[k * GROUPS + g, r - 1] = both.astype(jnp.bfloat16)
                c2_copy(k, g, r).start()

    def c_third(g, k):
        with scope(f"c_third{g}"):
            at = quarter(y)
            both = sums[k, core, g, at] + pair_in[k, g, at]
            c2_arrival(k, g).wait_recv()
            for r in range(1, ys):
                both = both + ring_in[k * GROUPS + g, r - 1].astype(jnp.float32)
            gate, up = both[:, :nc], both[:, nc:]
            hidden[g, own_slot, :, units(k)] = (gate / (1.0 + jnp.exp(-gate)) * up).astype(jnp.bfloat16)
            for r in range(1, ys):
                c3_copy(k, g, r, y).start()
            c4_copy(k, g, y).start()

    def c_fourth(g, k):
        with scope(f"c_fourth{g}"):
            for r in range(1, ys):
                c3_copy(k, g, r, y_at(-r)).wait_recv()
                c4_copy(k, g, y_at(-r)).start()

    def pipeline(steps, stages):
        def step(t, _):
            for lag, count, stage in stages:
                @pl.when(jnp.logical_and(t >= lag, t < count + lag))
                def _():
                    stage(t - lag)

            return 0

        lax.fori_loop(0, steps, step, 0)

    late = min(LATE, chunks)
    second, third, fourth = (
        [functools.partial(stage, g) for g in range(GROUPS)] for stage in (c_second, c_third, c_fourth)
    )
    pipeline(
        chunks + LAG_FORWARD,
        (
            (0, chunks, c_first),
            (LAG_SUM[0], chunks, second[0]),
            (LAG_SUM[1], chunks, second[1]),
            (LAG_HIDDEN[0], chunks, third[0]),
            (LAG_HIDDEN[1], chunks, third[1]),
            (LAG_FORWARD, chunks, fourth[0]),
            (LAG_FORWARD + late, chunks - late, fourth[1]),
        ),
    )

    def cols(n):
        return pl.ds(pl.multiple_of(n * cc, cc), cc)

    def d1_copy(job):
        return send(cross_out.at[job], cross_in.at[job], d1_send.at[0], d1_recv.at[job], x_peer)

    def d2_copy(job, n, b, r):
        return send(line_out.at[job, b], line_in.at[n, r - 1], d2_send.at[0], d2_recv.at[n], z_peer(r))

    def d2_arrival(n):
        return send(line_in.at[n], line_in.at[n], d2_send.at[0], d2_recv.at[n], z_peer(1))

    def d_first(job):
        g, n = lax.div(job, columns), lax.rem(job, columns)

        @pl.when(n == 0)
        def _():
            with scope("c4_wait"):
                c4_arrival(g).wait_recv()

        with scope("d_first"):
            rows = hidden[g].reshape(PAIR * gh, chunks * nc)
            product = jnp.dot(rows, down_v[:, cols(n)], preferred_element_type=jnp.float32)
            own[job] = product[:gh]
            cross_out[job] = product[gh:].astype(jnp.bfloat16)
            d1_copy(job).start()

    def d_second(job):
        g, n = lax.div(job, columns), lax.rem(job, columns)
        with scope("d_second"):
            d1_copy(job).wait_recv()
            summed = (own[job] + cross_in[job].astype(jnp.float32)).reshape(zb, tok, cc)
            cross_sum[job] = summed
            line_out[job] = summed.astype(jnp.bfloat16)
            for b in range(zb):
                r = lax.rem(zb * b + lax.rem(b + g, GROUPS) - z + zs, zs)

                @pl.when(r > 0)
                def _():
                    d2_copy(job, n, b, r).start()

    def d_third(job):
        g, n = lax.div(job, columns), lax.rem(job, columns)

        @pl.when(g == own_group)
        def _():
            with scope("d_third"):
                mlp_out = cross_sum[job, z_half]
                d2_arrival(n).wait_recv()
                for r in range(1, zs):
                    mlp_out = mlp_out + line_in[n, r - 1].astype(jnp.float32)
                for i in range(streams):
                    value = mixed[i, :, cols(n)] + column(post[i], 0) * mlp_out
                    out_ref[i, :, cols(n)] = value.astype(jnp.bfloat16)
                pltpu.make_async_copy(out_ref.at[:, :, cols(n)], out_hbm.at[:, :, cols(n)], out_sem.at[0]).start()

    jobs = GROUPS * columns
    pipeline(
        jobs + LAG_OUT,
        (
            (LAG_CROSS, jobs, d_second),
            (0, jobs, d_first),
            (1, late, lambda k: c_fourth(1, k + chunks - late)),
            (LAG_OUT, jobs, d_third),
        ),
    )

    with scope("drain"):
        a_all().wait_send()
        bx_all().wait_send()
        whole = [
            (rows_all.at[pl.ds(0, zs - 1)], bz_send),
            (pair_in, c1_send),
            (ring_in, c2_send),
            (hidden.at[:, pl.ds(0, ys - 1)], c3_send),
            (hidden.at[:, pl.ds(0, ys)], c4_send),
            (cross_in, d1_send),
            (line_in, d2_send),
        ]
        for ref, sem in whole:
            send(ref, ref, sem.at[0], sem.at[0], x_peer).wait_send()
        pltpu.make_async_copy(out_ref, out_hbm, out_sem.at[0]).wait()


def layer_scratch(zs, ys, tensors, tok, streams, logits, width, units, nc, cc):
    zb = zs // GROUPS
    gh = zb * tok
    gq = gh // ys
    chunks, columns = units // nc, width // cc
    jobs = GROUPS * columns
    f32, bf16 = jnp.float32, jnp.bfloat16
    arrays = [
        ((streams, tok, width), bf16),
        ((units, width), bf16),
        ((units, width), bf16),
        ((units, width), bf16),
        ((tok, streams, width), bf16),
        ((logits, streams, width), bf16),
        ((streams, tok, width), bf16),
        ((streams, logits, width), bf16),
        ((tok, LANES), f32),
        ((tensors - 1, tok, LANES), f32),
        ((tok, LANES), f32),
        ((streams, tok, LANES), f32),
        ((PAIR * zs, tok, width), bf16),
        ((streams, tok, width), f32),
        ((chunks, PAIR, GROUPS, gh, 2 * nc), f32),
        ((chunks, GROUPS, gh, 2 * nc), f32),
        ((chunks * GROUPS, ys - 1, gq, 2 * nc), bf16),
        ((chunks * GROUPS, ys - 1, gq, 2 * nc), bf16),
        ((GROUPS, PAIR * ys, gq, units), bf16),
        ((jobs, gh, cc), f32),
        ((jobs, gh, cc), bf16),
        ((jobs, gh, cc), bf16),
        ((jobs, zb, tok, cc), f32),
        ((jobs, zb, tok, cc), bf16),
        ((columns, zs - 1, tok, cc), bf16),
    ]
    sems = [(2,), (3,), (1,)]
    for count in (1, zs, 1, chunks, chunks * GROUPS, chunks * GROUPS * (ys - 1), GROUPS, jobs, columns):
        sems += [(1,), (count,)]
    size = sum(math.prod(shape) * jnp.dtype(kind).itemsize for shape, kind in arrays)
    return arrays, sems, size


def fused(mesh, streams, mix_weight, mix_bias, gate_weight, up_weight, down_weight):
    tok, stream_count, width = streams.shape
    units = gate_weight.shape[0]
    dps, tensors = mesh.shape["dp"], mesh.shape["tensor"]
    zs, ys = dps // PAIR, tensors // PAIR
    nc, cc = UNIT_CHUNK, COLUMN_CHUNK
    arrays, sems, _ = layer_scratch(zs, ys, tensors, tok, stream_count, mix_weight.shape[0], width, units, nc, cc)
    plan = (zs, ys, tensors, units // nc, nc, width // cc, cc, stream_count * width * tensors)
    bias = mix_bias[None, :]
    vmem = pl.BlockSpec(memory_space=pltpu.VMEM)
    hbm = pl.BlockSpec(memory_space=pl.ANY)
    out = pl.pallas_call(
        functools.partial(layer_kernel, plan),
        out_shape=jax.ShapeDtypeStruct((stream_count, tok, width), jnp.bfloat16),
        in_specs=[hbm, hbm, vmem, hbm, hbm, hbm],
        out_specs=hbm,
        scratch_shapes=[pltpu.VMEM(shape, kind) for shape, kind in arrays]
        + [pltpu.SemaphoreType.DMA(shape) for shape in sems],
        compiler_params=pltpu.CompilerParams(
            collective_id=0, has_side_effects=True, vmem_limit_bytes=VMEM_BUDGET
        ),
    )(streams, mix_weight, bias, gate_weight, up_weight, down_weight)
    return out.transpose(1, 0, 2)


def fits(mesh, streams, mix_weight, gate_weight):
    tok, stream_count, width = streams.shape
    units = gate_weight.shape[0]
    dps, tensors = mesh.shape["dp"], mesh.shape["tensor"]
    if dps != PAIR * GROUPS * PAIR or tensors % PAIR or tensors < 2 * PAIR:
        return False
    zs, ys = dps // PAIR, tensors // PAIR
    if units % UNIT_CHUNK or width % COLUMN_CHUNK or tok % 16 or (zs // GROUPS * tok) % (16 * ys):
        return False
    if mix_weight.shape[0] >= LANES:
        return False
    size = layer_scratch(
        zs, ys, tensors, tok, stream_count, mix_weight.shape[0], width, units, UNIT_CHUNK, COLUMN_CHUNK
    )[2]
    return size < VMEM_BUDGET * 3 // 4


def solution(mesh):
    in_specs = (
        P("dp", None, "tensor"),
        P(None, None, "tensor"),
        P(),
        P("dp", "tensor"),
        P("dp", "tensor"),
        P("dp", "tensor"),
    )
    out_specs = P("dp", None, "tensor")

    def step(streams, mix_weight, mix_bias, gate_weight, up_weight, down_weight):
        operands = (streams, mix_weight, mix_bias, gate_weight, up_weight, down_weight)
        if fits(mesh, streams, mix_weight, gate_weight):
            return fused(mesh, *operands)
        return per_device(*operands)

    return jax.shard_map(step, mesh=mesh, in_specs=in_specs, out_specs=out_specs, check_vma=False)
```

time: 52.1 us -> 46.8 us (0.90)
  Pallas kernels: 50.2 us -> 44.9 us
    pallas_call x1, Pallas kernels: 50.2 us -> 44.9 us  [fused(): pl.pallas_call(functools.partial(layer_kernel, plan), out_shape=jax.Shape...]
where the time goes in v2:
time: 46.8 us; the launch traced here: 46.7 us
  Pallas kernels  44.9 us (96%)
  local copies, waits for them, and re-layouts  1.75 us (4%)
    pallas_call x1, Pallas kernels, fused(): pl.pallas_call(functools.partial(layer_kernel, plan), out_shape=jax.Shape...  44.9 us
    transpose x1, local copies, waits for them, and re-layouts, fused(): return out.transpose(1, 0, 2)  1.75 us

profile of v2, /device:TPU:0, one launch (start us, length us, event | category | flops | bytes accessed | tf_op | source)
XLA Modules:
  0.0 46.7 jit_solution(5451067744257589537)
XLA Ops:
  0.0 44.9 %shard_map.64 = bf16[4,16,1792]{2,1,0:T(8,128)(2,1)} custom-call(bf16[16,4,1792]{2,1,0:T(4,128)(2,1)} %s_hbm.1, bf16[24,4,1792]{2,1,0:T(4,128)(2,1)} %mw_hbm.1, f32[1,24]{1,0:T(1,128)} %bitcast.3, bf16[2304,1792]{1,0:T(8,128)(2,1)} %gate_hbm.1, bf16[2304,1792]{1,0:T(8,128)(2,1)} %up_hbm.1, bf16[2304,1792]{1,0:T(8,128)(2,1)} %down_hbm.1), custom_call_target="tpu_custom_call" | custom-call | tf_op jit(solution)/shard_map/pallas_call | solution.py:583
  44.9 1.7 %copy.7 = bf16[16,4,1792]{2,1,0:T(4,128)(2,1)} copy(bf16[16,4,1792]{2,0,1:T(8,128)(2,1)} %bitcast.2) | data formatting | bytes 458752 | tf_op jit(solution)/shard_map/transpose | solution.py:594

commit v3 on v2

--- a/solution.py
+++ b/solution.py
@@ -86,7 +86,7 @@
 LATE = 4
 LAG_CROSS = 7
 LAG_OUT = 21
-TURNS = (6, 4, 4)
+TURNS = (8, 3, 2)
 VMEM_BUDGET = 58 * 1024 * 1024
 
 
@@ -125,7 +125,6 @@
     gate_hbm,
     up_hbm,
     down_hbm,
-    out_hbm,
     out_ref,
     gate_v,
     up_v,
@@ -153,7 +152,6 @@
     line_in,
     in_sem,
     w_sem,
-    out_sem,
     a_send,
     a_recv,
     bz_send,
@@ -464,12 +462,29 @@
             with scope("c4_wait"):
                 c4_arrival(g).wait_recv()
 
-        with scope("d_first"):
+        def product(offset):
             rows = hidden[g].reshape(PAIR * gh, chunks * nc)
-            product = jnp.dot(rows, down_v[:, cols(n)], preferred_element_type=jnp.float32)
-            own[job] = product[:gh]
-            cross_out[job] = product[gh:].astype(jnp.bfloat16)
-            d1_copy(job).start()
+            return jnp.dot(rows, down_v[:, cols(n + offset)], preferred_element_type=jnp.float32)
+
+        def finish(offset, value):
+            own[job + offset] = value[:gh]
+            cross_out[job + offset] = value[gh:].astype(jnp.bfloat16)
+            d1_copy(job + offset).start()
+
+        paired = columns // PAIR * PAIR
+
+        @pl.when(jnp.logical_and(n < paired, lax.rem(n, PAIR) == 0))
+        def _():
+            with scope("d_first_pair"):
+                values = [product(offset) for offset in range(PAIR)]
+                for offset in range(PAIR):
+                    finish(offset, values[offset])
+
+        if paired < columns:
+            @pl.when(n >= paired)
+            def _():
+                with scope("d_first"):
+                    finish(0, product(0))
 
     def d_second(job):
         g, n = lax.div(job, columns), lax.rem(job, columns)
@@ -498,7 +513,6 @@
                 for i in range(streams):
                     value = mixed[i, :, cols(n)] + column(post[i], 0) * mlp_out
                     out_ref[i, :, cols(n)] = value.astype(jnp.bfloat16)
-                pltpu.make_async_copy(out_ref.at[:, :, cols(n)], out_hbm.at[:, :, cols(n)], out_sem.at[0]).start()
 
     jobs = GROUPS * columns
     pipeline(
@@ -525,7 +539,6 @@
         ]
         for ref, sem in whole:
             send(ref, ref, sem.at[0], sem.at[0], x_peer).wait_send()
-        pltpu.make_async_copy(out_ref, out_hbm, out_sem.at[0]).wait()
 
 
 def layer_scratch(zs, ys, tensors, tok, streams, logits, width, units, nc, cc):
@@ -536,7 +549,6 @@
     jobs = GROUPS * columns
     f32, bf16 = jnp.float32, jnp.bfloat16
     arrays = [
-        ((streams, tok, width), bf16),
         ((units, width), bf16),
         ((units, width), bf16),
         ((units, width), bf16),
@@ -562,7 +574,7 @@
         ((jobs, zb, tok, cc), bf16),
         ((columns, zs - 1, tok, cc), bf16),
     ]
-    sems = [(2,), (3,), (1,)]
+    sems = [(2,), (3,)]
     for count in (1, zs, 1, chunks, chunks * GROUPS, chunks * GROUPS * (ys - 1), GROUPS, jobs, columns):
         sems += [(1,), (count,)]
     size = sum(math.prod(shape) * jnp.dtype(kind).itemsize for shape, kind in arrays)
@@ -582,9 +594,9 @@
     hbm = pl.BlockSpec(memory_space=pl.ANY)
     out = pl.pallas_call(
         functools.partial(layer_kernel, plan),
-        out_shape=jax.ShapeDtypeStruct((stream_count, tok, width), jnp.bfloat16),
+        out_shape=pltpu.VMEM((stream_count, tok, width), jnp.bfloat16),
         in_specs=[hbm, hbm, vmem, hbm, hbm, hbm],
-        out_specs=hbm,
+        out_specs=vmem,
         scratch_shapes=[pltpu.VMEM(shape, kind) for shape, kind in arrays]
         + [pltpu.SemaphoreType.DMA(shape) for shape in sems],
         compiler_params=pltpu.CompilerParams(

time: 46.8 us -> 45.3 us (0.968)
  local copies, waits for them, and re-layouts: 1.75 us -> 0.81 us
  Pallas kernels: 44.9 us -> 44.3 us
    transpose x1, local copies, waits for them, and re-layouts: 1.75 us -> 0.81 us  [fused(): return out.transpose(1, 0, 2)]
    pallas_call x1, Pallas kernels: 44.9 us -> 44.3 us  [fused(): pl.pallas_call(functools.partial(layer_kernel, plan), out_shape=pltpu.VME...]
where the time goes in v3:
time: 45.3 us; the launch traced here: 45.1 us
  Pallas kernels  44.3 us (98%)
  local copies, waits for them, and re-layouts  0.81 us (2%)
    pallas_call x1, Pallas kernels, fused(): pl.pallas_call(functools.partial(layer_kernel, plan), out_shape=pltpu.VME...  44.3 us

profile of v3, /device:TPU:0, one launch (start us, length us, event | category | flops | bytes accessed | tf_op | source)
XLA Modules:
  0.0 45.1 jit_solution(444822425063140007)
XLA Ops:
  0.0 44.3 %shard_map.64 = bf16[4,16,1792]{2,1,0:T(8,128)(2,1)S(1)} custom-call(bf16[16,4,1792]{2,1,0:T(4,128)(2,1)} %s_hbm.1, bf16[24,4,1792]{2,1,0:T(4,128)(2,1)} %mw_hbm.1, f32[1,24]{1,0:T(1,128)} %bitcast.3, bf16[2304,1792]{1,0:T(8,128)(2,1)} %gate_hbm.1, bf16[2304,1792]{1,0:T(8,128)(2,1)} %up_hbm.1, bf16[2304,1792]{1,0:T(8,128)(2,1)} %down_hbm.1), custom_call_target="tpu_custom_call" | custom-call | tf_op jit(solution)/shard_map/pallas_call | solution.py:595
  44.3 0.8 %copy.7 = bf16[16,4,1792]{2,1,0:T(4,128)(2,1)} copy(bf16[16,4,1792]{2,0,1:T(8,128)(2,1)S(1)} %bitcast.2) | data formatting | bytes 458752 | tf_op jit(solution)/shard_map/transpose | solution.py:606

commit v4 on v2

v4 whole, which is shorter than its diff:
```python
import functools
import math

import jax
import jax.numpy as jnp
from jax import lax
from jax.experimental import pallas as pl
from jax.experimental.pallas import tpu as pltpu
from jax.sharding import PartitionSpec as P

D = 7168
ITERS = 20


epsilon = 1e-06


def normalize(sweep_index, matrix):
    matrix = matrix / jnp.sum(matrix, axis=2, keepdims=True)
    return matrix / jnp.sum(matrix, axis=1, keepdims=True)


def mixing(raw_logits, squares, mix_bias, stream_count):
    scale_inv = lax.rsqrt(squares / (stream_count * D) + epsilon)
    logits = raw_logits * scale_inv[:, None] + mix_bias[None, :]
    pre_gate = jax.nn.sigmoid(logits[:, :stream_count])
    post_gate = 2.0 * jax.nn.sigmoid(logits[:, stream_count : 2 * stream_count])
    matrix = jnp.exp(logits[:, 2 * stream_count :]).reshape(-1, stream_count, stream_count)
    matrix = lax.fori_loop(0, ITERS, normalize, matrix)
    return (pre_gate, post_gate, matrix)


def contract_last(weights, rows):
    return lax.dot_general(
        weights, rows, (((1,), (1,)), ((), ())), preferred_element_type=jnp.float32
    )


def per_device(streams, mix_weight, mix_bias, gate_weight, up_weight, down_weight):
    tok_rows, stream_count, width_local = streams.shape
    logit_count = mix_weight.shape[0]
    flat_rows = streams.reshape(tok_rows, stream_count * width_local)
    flat_weight = mix_weight.reshape(logit_count, stream_count * width_local)
    raw_logits = lax.dot_general(
        flat_rows, flat_weight, (((1,), (1,)), ((), ())), preferred_element_type=jnp.float32
    )
    stream_wide = streams.astype(jnp.float32)
    squares = jnp.sum(stream_wide * stream_wide, axis=(1, 2))
    total_logits, total_squares = lax.psum((raw_logits, squares), "tensor")
    pre_gate, post_gate, res_mix = mixing(total_logits, total_squares, mix_bias, stream_count)
    mlp_input = jnp.einsum(
        "ts,tsc->tc", pre_gate, stream_wide, precision=lax.Precision.HIGHEST
    ).astype(jnp.bfloat16)
    unit_local = gate_weight.shape[0]
    block_rows = lax.all_gather(mlp_input, "dp", axis=0, tiled=True)
    gate_part = contract_last(gate_weight, block_rows)
    up_part = contract_last(up_weight, block_rows)
    both_parts = jnp.concatenate((gate_part, up_part), axis=0)
    unit_share = lax.psum_scatter(both_parts, "tensor", scatter_dimension=1, tiled=True)
    hidden_share = (jax.nn.silu(unit_share[:unit_local]) * unit_share[unit_local:]).astype(
        jnp.bfloat16
    )
    hidden = lax.all_gather(hidden_share, "tensor", axis=1, tiled=True)
    mlp_out = lax.psum_scatter(
        lax.dot_general(
            hidden, down_weight, (((0,), (0,)), ((), ())), preferred_element_type=jnp.float32
        ),
        "dp",
        scatter_dimension=0,
        tiled=True,
    )
    mixed = jnp.einsum("tij,tjc->tic", res_mix, stream_wide, precision=lax.Precision.HIGHEST)
    mixed = mixed + post_gate[:, :, None] * mlp_out[:, None, :]
    return mixed.astype(jnp.bfloat16)


MESH = pl.DeviceIdType.MESH
UNIT_CHUNK = 256
COLUMN_CHUNK = 256
PAIR = 2
GROUPS = 2
BODY = 3
LANES = 128
SUM_AT, HIDDEN_AT, FORWARD_AT = 1.99, 4.3, 6.5
FAR_GAP = 1.4
NEAR_DOWN = (10.75, 10.8, 11.0, 11.5)
VMEM_BUDGET = 58 * 1024 * 1024


def column(values, at):
    return values[:, at : at + 1]


def sigmoid(v):
    return 1.0 / (1.0 + jnp.exp(-v))


def sweep(count, _, entries):
    m = list(entries)
    for i in range(count):
        total_row = m[i * count]
        for j in range(1, count):
            total_row = total_row + m[i * count + j]
        inv = 1.0 / total_row
        for j in range(count):
            m[i * count + j] = m[i * count + j] * inv
    for j in range(count):
        total_col = m[j]
        for i in range(1, count):
            total_col = total_col + m[i * count + j]
        inv = 1.0 / total_col
        for i in range(count):
            m[i * count + j] = m[i * count + j] * inv
    return tuple(m)


def layer_kernel(
    plan,
    s_hbm,
    mw_hbm,
    bias_ref,
    gate_hbm,
    up_hbm,
    down_hbm,
    out_ref,
    gate_v,
    up_v,
    down_v,
    s_raw,
    mw_raw,
    s_ref,
    mw_ref,
    part,
    part_in,
    entry,
    logit_ref,
    post,
    rows_all,
    mixed,
    sums,
    pair_in,
    ring_out,
    ring_in,
    hidden,
    own,
    cross_out,
    cross_in,
    cross_sum,
    line_out,
    line_in,
    in_sem,
    w_sem,
    a_send,
    a_recv,
    bz_send,
    bz_recv,
    bx_send,
    bx_recv,
    c1_send,
    c1_recv,
    c2_send,
    c2_recv,
    c3_send,
    c3_recv,
    c4_send,
    c4_recv,
    d1_send,
    d1_recv,
    d2_send,
    d2_recv,
):
    zs, ys, tensors, chunks, nc, columns, cc, width_all = plan
    streams, tok, width = s_ref.shape
    scope = jax.named_scope
    dp = lax.axis_index("dp")
    tp = lax.axis_index("tensor")
    z, x = lax.div(dp, PAIR), lax.rem(dp, PAIR)
    y, core = lax.div(tp, PAIR), lax.rem(tp, PAIR)
    x_peer = (z * PAIR + 1 - x, tp)
    core_peer = (dp, y * PAIR + 1 - core)
    zb = zs // GROUPS
    gh = zb * tok
    gq = gh // ys
    z_half, z_odd = lax.div(z, zb), lax.rem(z, zb)

    def slot_of(source, target):
        apart = lax.rem(lax.div(source, zb) + lax.div(target, zb), GROUPS)
        return apart * PAIR * zb + lax.rem(source, zb)

    def y_at(r):
        return lax.rem(y + r + ys, ys)

    def z_dev(at):
        return (at * PAIR + x, tp)

    def z_peer(r):
        return z_dev(lax.rem(z + r + zs, zs))

    def block_peer(across, apart):
        at = z_half * zb + lax.rem(z_odd + apart, zb)
        return (at * PAIR + lax.rem(x + across, PAIR), tp)

    def y_peer(r):
        return (dp, y_at(r) * PAIR + core)

    def t_peer(r):
        return (dp, lax.rem(tp + r, tensors))

    def send(src, dst, ssem, rsem, peer):
        return pltpu.make_async_remote_copy(
            src_ref=src, dst_ref=dst, send_sem=ssem, recv_sem=rsem, device_id=peer, device_id_type=MESH
        )

    weights = ((gate_hbm, gate_v), (up_hbm, up_v), (down_hbm, down_v))

    def start_weights(k, _, which):
        hbm, vmem = weights[which]
        part_of = pl.ds(k * nc, nc)
        pltpu.make_async_copy(hbm.at[part_of], vmem.at[part_of], w_sem.at[which]).start()
        return 0

    def weight_wait(which):
        hbm, vmem = weights[which]
        pltpu.make_async_copy(hbm, vmem, w_sem.at[which]).wait()

    barrier = pltpu.get_barrier_semaphore()
    peers = [t_peer(r) for r in range(1, tensors)] + [x_peer, block_peer(1, 1)] + [z_peer(r) for r in range(1, zs)]
    with scope("start"):
        for peer in peers:
            pl.semaphore_signal(barrier, inc=1, device_id=peer, device_id_type=MESH)
        inputs = (
            pltpu.make_async_copy(s_hbm, s_raw, in_sem.at[0]),
            pltpu.make_async_copy(mw_hbm, mw_raw, in_sem.at[1]),
        )
        for copy in inputs:
            copy.start()
        for which in range(3):
            lax.fori_loop(0, chunks, functools.partial(start_weights, which=which), 0)
        for copy in inputs:
            copy.wait()
    with scope("relayout"):
        for j in range(streams):
            s_ref[j] = s_raw[:, j, :]
            mw_ref[j] = mw_raw[:, j, :]

    with scope("raw_logits"):
        raw = jnp.zeros((tok, mw_ref.shape[1]), jnp.float32)
        squares = jnp.zeros((tok, 1), jnp.float32)
        for j in range(streams):
            raw += contract_last(s_ref[j], mw_ref[j])
            wide = s_ref[j].astype(jnp.float32)
            squares += jnp.sum(wide * wide, axis=1, keepdims=True)
        count = raw.shape[1]
        part[...] = jnp.broadcast_to(squares, part.shape)
        part[:, :count] = raw
    with scope("barrier"):
        pl.semaphore_wait(barrier, len(peers))

    def a_copy(r):
        return send(part, part_in.at[r - 1], a_send.at[0], a_recv.at[0], t_peer(r))

    def a_all():
        return send(part_in, part_in, a_send.at[0], a_recv.at[0], t_peer(1))

    with scope("a_exchange"):
        for r in range(1, tensors):
            a_copy(r).start()
        a_all().wait_recv()
    with scope("gates"):
        total = part[...]
        for r in range(1, tensors):
            total = total + part_in[r - 1]
        scale_inv = lax.rsqrt(column(total, count) / width_all + epsilon)
        logits = total[:, :count] * scale_inv + bias_ref[...]
        logit_ref[:, :count] = logits
        gates = sigmoid(logits)
        mlp_input = column(gates, 0) * s_ref[0].astype(jnp.float32)
        for j in range(1, streams):
            mlp_input += column(gates, j) * s_ref[j].astype(jnp.float32)
        rows_all[slot_of(z, z)] = mlp_input.astype(jnp.bfloat16)

    mate, inner, outer = z_half * zb + 1 - z_odd, zb - z_half, (zs - 1) * (1 - z_half)

    def bz_copy(source, target):
        src, dst = rows_all.at[slot_of(source, source)], rows_all.at[slot_of(source, target)]
        return send(src, dst, bz_send.at[0], bz_recv.at[source], z_dev(target))

    def bz_arrival(source):
        block = rows_all.at[slot_of(source, z)]
        return send(block, block, bz_send.at[0], bz_recv.at[source], z_dev(source))

    def bx_copy(source, g):
        at = slot_of(source, z)
        return send(rows_all.at[at], rows_all.at[at + zb], bx_send.at[0], bx_recv.at[g], x_peer)

    def bx_all(g):
        received = rows_all.at[pl.ds((g * PAIR + 1) * zb, zb)]
        return send(received, received, bx_send.at[0], bx_recv.at[g], x_peer)

    def bx_mate():
        src, dst = rows_all.at[slot_of(z, z)], rows_all.at[slot_of(z, mate) + zb]
        return send(src, dst, bx_send.at[0], bx_recv.at[0], block_peer(1, 1))

    with scope("b_start"):
        bz_copy(z, mate).start()
        bx_mate().start()
        bx_copy(z, 0).start()
        for target in (outer, inner):
            bz_copy(z, target).start()
        for i in range(streams):
            post[i] = jnp.broadcast_to(2.0 * column(gates, streams + i), (tok, post.shape[2]))

    def turn(k, _, which):
        with scope("turn"):
            vmem = weights[which][1]
            span = pl.ds(pl.multiple_of(k * nc, nc), nc)
            for at in range(0, width, nc):
                vmem[span, at : at + nc] = vmem[span, at : at + nc].T
        return 0

    for which in range(2):
        weight_wait(which)
        lax.fori_loop(0, chunks, functools.partial(turn, which=which), 0)
    with scope("b_wait"):
        bz_arrival(mate).wait_recv()
        bx_all(0).wait_recv()

    def forward(_):
        with scope("b_forward"):
            for source in (inner, outer):
                bz_arrival(source).wait_recv()
                bx_copy(source, 1).start()

    def streams_mixed(_):
        with scope("sinkhorn"):
            entry[...] = jnp.zeros_like(entry)
            entry[:, :count] = jnp.exp(logit_ref[:, :count])
            flipped = entry[...].T
            first = 2 * streams
            mat = tuple(flipped[first + at : first + at + 1] for at in range(streams * streams))
            mat = lax.fori_loop(0, ITERS, functools.partial(sweep, streams), mat)
        with scope("mixed"):
            rest = jnp.zeros((LANES - len(mat), tok), jnp.float32)
            res = jnp.concatenate(mat + (rest,), axis=0).T
            for i in range(streams):
                line = column(res, i * streams) * s_ref[0].astype(jnp.float32)
                for j in range(1, streams):
                    line += column(res, i * streams + j) * s_ref[j].astype(jnp.float32)
                mixed[i] = line

    own_slot = core * ys + y

    def units(job):
        return pl.ds(pl.multiple_of(lax.rem(job, chunks) * nc, nc), nc)

    def quarter(at):
        return pl.ds(pl.multiple_of(at * gq, gq), gq)

    def c1_copy(job):
        span = pl.ds(job, BODY)
        return send(sums.at[span, 1 - core], pair_in.at[span], c1_send.at[0], c1_recv.at[lax.div(job, BODY)], core_peer)

    def c2_copy(job, r):
        return send(ring_out.at[job, r - 1], ring_in.at[job, r - 1], c2_send.at[0], c2_recv.at[job], y_peer(r))

    def c2_arrival(job):
        return send(ring_in.at[job], ring_in.at[job], c2_send.at[0], c2_recv.at[job], y_peer(1))

    def c3_copy(job, r, source):
        piece = hidden.at[lax.div(job, chunks), core * ys + source, :, units(job)]
        return send(piece, piece, c3_send.at[0], c3_recv.at[job * (ys - 1) + r - 1], y_peer(r))

    def c4_copy(job, source):
        g = lax.div(job, chunks)
        piece = hidden.at[g, core * ys + source, :, units(job)]
        return send(piece, piece, c4_send.at[0], c4_recv.at[g], core_peer)

    def c4_arrival(g):
        piece = hidden.at[g, pl.ds((1 - core) * ys, ys)]
        return send(piece, piece, c4_send.at[0], c4_recv.at[g], core_peer)

    def far_wait(_):
        with scope("far_wait"):
            bx_all(1).wait_recv()

    def c_first(job):
        with scope("c_first"):
            g = job // chunks
            rows = rows_all[pl.ds(g * PAIR * zb, PAIR * zb)].reshape(PAIR * gh, width)
            for i in range(BODY):
                for at, vmem in ((pl.ds(0, nc), gate_v), (pl.ds(nc, nc), up_v)):
                    product = None
                    for kt in range(0, width, nc):
                        block = vmem[units(job + i), kt : kt + nc]
                        term = jnp.dot(rows[:, kt : kt + nc], block, preferred_element_type=jnp.float32)
                        product = term if product is None else product + term
                    sums[job + i, :, :, at] = product.reshape(PAIR, gh, nc)
            c1_copy(job).start()

    def c_second(job):
        with scope("c_second"):
            for r in range(1, ys):
                at = quarter(y_at(r))
                both = sums[job, core, at] + pair_in[job, at]
                ring_out[job, r - 1] = both.astype(jnp.bfloat16)
                c2_copy(job, r).start()

    def c_third(job):
        with scope("c_third"):
            at = quarter(y)
            both = sums[job, core, at] + pair_in[job, at]
            c2_arrival(job).wait_recv()
            for r in range(1, ys):
                both = both + ring_in[job, r - 1].astype(jnp.float32)
            gate, up = both[:, :nc], both[:, nc:]
            g = lax.div(job, chunks)
            hidden[g, own_slot, :, units(job)] = (gate / (1.0 + jnp.exp(-gate)) * up).astype(jnp.bfloat16)
            for r in range(1, ys):
                c3_copy(job, r, y).start()
            c4_copy(job, y).start()

    def c_fourth(job):
        with scope("c_fourth"):
            for r in range(1, ys):
                c3_copy(job, r, y_at(-r)).wait_recv()
                c4_copy(job, y_at(-r)).start()

    def run(stage, first, count):
        def body(job, _):
            stage(job)
            return 0

        lax.fori_loop(first, first + count, body, 0)

    def cols(n):
        return pl.ds(pl.multiple_of(n * cc, cc), cc)

    def d1_copy(job, r):
        across, apart = r // zb, r % zb
        piece = cross_out.at[job, across * zb + lax.rem(z_odd + apart, zb)]
        return send(piece, cross_in.at[job, r - 1], d1_send.at[0], d1_recv.at[job], block_peer(across, apart))

    def d1_arrival(job):
        return send(cross_in.at[job], cross_in.at[job], d1_send.at[0], d1_recv.at[job], x_peer)

    def d2_copy(n):
        return send(line_out.at[n], line_in.at[n], d2_send.at[0], d2_recv.at[n], z_peer(zb))

    def d_first(g, n, width_of):
        with scope("d_first"):
            rows = hidden[g].reshape(PAIR * gh, chunks * nc)
            values = [
                jnp.dot(rows, down_v[:, (n + i) * cc : (n + i + 1) * cc], preferred_element_type=jnp.float32)
                for i in range(width_of)
            ]
            for i, value in enumerate(values):
                job = g * columns + n + i
                value = value.reshape(PAIR * zb, tok, cc)
                own[job] = value
                cross_out[job] = value.astype(jnp.bfloat16)
                for r in range(1, PAIR * zb):
                    d1_copy(job, r).start()

    alone = columns % PAIR
    parts = [(0, alone)] * (alone > 0) + [(n, PAIR) for n in range(alone, columns, PAIR)]

    def block_sum(job):
        total = own[job, z_odd]
        d1_arrival(job).wait_recv()
        for r in range(1, PAIR * zb):
            total = total + cross_in[job, r - 1].astype(jnp.float32)
        return total

    def d_near(n):
        with scope("d_near"):
            cross_sum[n] = block_sum(n)

    def d_far(n):
        with scope("d_far"):
            line_out[n] = block_sum(n + columns).astype(jnp.bfloat16)
            d2_copy(n).start()

    def d_third(n):
        with scope("d_third"):
            mlp_out = cross_sum[n]
            d2_copy(n).wait_recv()
            mlp_out = mlp_out + line_in[n].astype(jnp.float32)
            for i in range(streams):
                value = mixed[i, :, cols(n)] + column(post[i], 0) * mlp_out
                out_ref[i, :, cols(n)] = value.astype(jnp.bfloat16)

    def sum_triple(job):
        with scope("c1_wait"):
            c1_copy(job).wait_recv()
        run(c_second, job, BODY)

    def near_ready(_):
        with scope("c4_wait"):
            c4_arrival(0).wait_recv()
            weight_wait(2)

    triples = chunks // BODY
    base = triples + FAR_GAP
    timed = [(0.5, forward, 0), (triples + 0.2, streams_mixed, 0), (base - 0.01, far_wait, 0)]
    for g, origin in enumerate((0, base)):
        for i in range(triples):
            job = g * chunks + i * BODY
            timed += [
                (origin + i, c_first, job),
                (origin + i + SUM_AT, sum_triple, job),
                (origin + i + HIDDEN_AT, functools.partial(run, c_third, count=BODY), job),
                (origin + i + FORWARD_AT, functools.partial(run, c_fourth, count=BODY), job),
            ]
    for i, (n, count_of) in enumerate(parts):
        at = NEAR_DOWN[min(i, len(NEAR_DOWN) - 1)]
        if i == 0:
            timed.append((at - 0.01, near_ready, 0))
        timed.append((at, lambda _, n=n, count_of=count_of: d_first(0, n, count_of), 0))
    for _, stage, job in sorted(timed, key=lambda item: item[0]):
        if isinstance(stage, functools.partial):
            stage(first=job)
        else:
            stage(job)

    with scope("c4_wait"):
        c4_arrival(1).wait_recv()
    for n, count_of in parts:
        d_first(1, n, count_of)
    run(d_near, 0, columns)
    run(d_far, 0, columns)
    run(d_third, 0, columns)

    with scope("drain"):
        a_all().wait_send()
        for g in range(GROUPS):
            bx_all(g).wait_send()
        whole = [
            (rows_all.at[pl.ds(0, zs - 1)], bz_send),
            (pair_in, c1_send),
            (ring_in, c2_send),
            (hidden.at[:, pl.ds(0, ys - 1)], c3_send),
            (hidden.at[:, pl.ds(0, ys)], c4_send),
            (cross_in, d1_send),
            (line_in, d2_send),
        ]
        for ref, sem in whole:
            send(ref, ref, sem.at[0], sem.at[0], x_peer).wait_send()


def layer_scratch(zs, ys, tensors, tok, streams, logits, width, units, nc, cc):
    zb = zs // GROUPS
    gh = zb * tok
    gq = gh // ys
    chunks, columns = units // nc, width // cc
    jobs = GROUPS * columns
    f32, bf16 = jnp.float32, jnp.bfloat16
    arrays = [
        ((units, width), bf16),
        ((units, width), bf16),
        ((units, width), bf16),
        ((tok, streams, width), bf16),
        ((logits, streams, width), bf16),
        ((streams, tok, width), bf16),
        ((streams, logits, width), bf16),
        ((tok, LANES), f32),
        ((tensors - 1, tok, LANES), f32),
        ((tok, LANES), f32),
        ((tok, LANES), f32),
        ((streams, tok, LANES), f32),
        ((PAIR * zs, tok, width), bf16),
        ((streams, tok, width), f32),
        ((chunks * GROUPS, PAIR, gh, 2 * nc), f32),
        ((chunks * GROUPS, gh, 2 * nc), f32),
        ((chunks * GROUPS, ys - 1, gq, 2 * nc), bf16),
        ((chunks * GROUPS, ys - 1, gq, 2 * nc), bf16),
        ((GROUPS, PAIR * ys, gq, units), bf16),
        ((jobs, PAIR * zb, tok, cc), f32),
        ((jobs, PAIR * zb, tok, cc), bf16),
        ((jobs, PAIR * zb - 1, tok, cc), bf16),
        ((columns, tok, cc), f32),
        ((columns, tok, cc), bf16),
        ((columns, tok, cc), bf16),
    ]
    sems = [(2,), (3,)]
    for count in (1, zs, GROUPS, chunks * GROUPS // BODY, chunks * GROUPS, chunks * GROUPS * (ys - 1), GROUPS, jobs, columns):
        sems += [(1,), (count,)]
    size = sum(math.prod(shape) * jnp.dtype(kind).itemsize for shape, kind in arrays)
    return arrays, sems, size


def fused(mesh, streams, mix_weight, mix_bias, gate_weight, up_weight, down_weight):
    tok, stream_count, width = streams.shape
    units = gate_weight.shape[0]
    dps, tensors = mesh.shape["dp"], mesh.shape["tensor"]
    zs, ys = dps // PAIR, tensors // PAIR
    nc, cc = UNIT_CHUNK, COLUMN_CHUNK
    arrays, sems, _ = layer_scratch(zs, ys, tensors, tok, stream_count, mix_weight.shape[0], width, units, nc, cc)
    plan = (zs, ys, tensors, units // nc, nc, width // cc, cc, stream_count * width * tensors)
    bias = mix_bias[None, :]
    vmem = pl.BlockSpec(memory_space=pltpu.VMEM)
    hbm = pl.BlockSpec(memory_space=pl.ANY)
    out = pl.pallas_call(
        functools.partial(layer_kernel, plan),
        out_shape=pltpu.VMEM((stream_count, tok, width), jnp.bfloat16),
        in_specs=[hbm, hbm, vmem, hbm, hbm, hbm],
        out_specs=vmem,
        scratch_shapes=[pltpu.VMEM(shape, kind) for shape, kind in arrays]
        + [pltpu.SemaphoreType.DMA(shape) for shape in sems],
        compiler_params=pltpu.CompilerParams(
            collective_id=0, has_side_effects=True, vmem_limit_bytes=VMEM_BUDGET
        ),
    )(streams, mix_weight, bias, gate_weight, up_weight, down_weight)
    return out.transpose(1, 0, 2)


def fits(mesh, streams, mix_weight, gate_weight):
    tok, stream_count, width = streams.shape
    units = gate_weight.shape[0]
    dps, tensors = mesh.shape["dp"], mesh.shape["tensor"]
    if dps != PAIR * GROUPS * PAIR or tensors % PAIR or tensors < 2 * PAIR:
        return False
    zs, ys = dps // PAIR, tensors // PAIR
    if units % (BODY * UNIT_CHUNK) or width % UNIT_CHUNK or width % COLUMN_CHUNK or tok % 16 or (zs // GROUPS * tok) % (16 * ys):
        return False
    if mix_weight.shape[0] >= LANES:
        return False
    size = layer_scratch(
        zs, ys, tensors, tok, stream_count, mix_weight.shape[0], width, units, UNIT_CHUNK, COLUMN_CHUNK
    )[2]
    return size < VMEM_BUDGET * 3 // 4


def solution(mesh):
    in_specs = (
        P("dp", None, "tensor"),
        P(None, None, "tensor"),
        P(),
        P("dp", "tensor"),
        P("dp", "tensor"),
        P("dp", "tensor"),
    )
    out_specs = P("dp", None, "tensor")

    def step(streams, mix_weight, mix_bias, gate_weight, up_weight, down_weight):
        operands = (streams, mix_weight, mix_bias, gate_weight, up_weight, down_weight)
        if fits(mesh, streams, mix_weight, gate_weight):
            return fused(mesh, *operands)
        return per_device(*operands)

    return jax.shard_map(step, mesh=mesh, in_specs=in_specs, out_specs=out_specs, check_vma=False)
```

time: 46.8 us -> 43.9 us (0.938)
  Pallas kernels: 44.9 us -> 42.9 us
  local copies, waits for them, and re-layouts: 1.75 us -> 0.81 us
    pallas_call x1, Pallas kernels: 44.9 us -> 42.9 us  [fused(): pl.pallas_call(functools.partial(layer_kernel, plan), out_shape=pltpu.VME...]
    transpose x1, local copies, waits for them, and re-layouts: 1.75 us -> 0.81 us  [fused(): return out.transpose(1, 0, 2)]
where the time goes in v4:
time: 43.9 us; the launch traced here: 43.7 us
  Pallas kernels  42.9 us (98%)
  local copies, waits for them, and re-layouts  0.81 us (2%)
    pallas_call x1, Pallas kernels, fused(): pl.pallas_call(functools.partial(layer_kernel, plan), out_shape=pltpu.VME...  42.9 us

profile of v4, /device:TPU:0, one launch (start us, length us, event | category | flops | bytes accessed | tf_op | source)
XLA Modules:
  0.0 43.7 jit_solution(4898109854025880331)
XLA Ops:
  0.0 42.9 %shard_map.64 = bf16[4,16,1792]{2,1,0:T(8,128)(2,1)S(1)} custom-call(bf16[16,4,1792]{2,1,0:T(4,128)(2,1)} %s_hbm.1, bf16[24,4,1792]{2,1,0:T(4,128)(2,1)} %mw_hbm.1, f32[1,24]{1,0:T(1,128)} %bitcast.3, bf16[2304,1792]{1,0:T(8,128)(2,1)} %gate_hbm.1, bf16[2304,1792]{1,0:T(8,128)(2,1)} %up_hbm.1, bf16[2304,1792]{1,0:T(8,128)(2,1)} %down_hbm.1), custom_call_target="tpu_custom_call" | custom-call | tf_op jit(solution)/shard_map/pallas_call | solution.py:602
  42.9 0.8 %copy.7 = bf16[16,4,1792]{2,1,0:T(4,128)(2,1)} copy(bf16[16,4,1792]{2,0,1:T(8,128)(2,1)S(1)} %bitcast.2) | data formatting | bytes 458752 | tf_op jit(solution)/shard_map/transpose | solution.py:613

commit v5 on v4

--- a/solution.py
+++ b/solution.py
@@ -81,9 +81,9 @@
 GROUPS = 2
 BODY = 3
 LANES = 128
-SUM_AT, HIDDEN_AT, FORWARD_AT = 1.99, 4.3, 6.5
-FAR_GAP = 1.4
-NEAR_DOWN = (10.75, 10.8, 11.0, 11.5)
+SUM_AT, HIDDEN_AT, FORWARD_AT = (0.99, 0.99), 3.3, 5.5
+NEAR_HIDDEN, NEAR_FORWARD = 4.1, 6.33
+FAR_GAP = 0.5
 VMEM_BUDGET = 58 * 1024 * 1024
 
 
@@ -303,10 +303,10 @@
 
     with scope("b_start"):
         bz_copy(z, mate).start()
-        bx_mate().start()
         bx_copy(z, 0).start()
         for target in (outer, inner):
             bz_copy(z, target).start()
+        bx_mate().start()
         for i in range(streams):
             post[i] = jnp.broadcast_to(2.0 * column(gates, streams + i), (tok, post.shape[2]))
 
@@ -321,15 +321,10 @@
     for which in range(2):
         weight_wait(which)
         lax.fori_loop(0, chunks, functools.partial(turn, which=which), 0)
-    with scope("b_wait"):
-        bz_arrival(mate).wait_recv()
-        bx_all(0).wait_recv()
-
-    def forward(_):
+    def forward(source):
         with scope("b_forward"):
-            for source in (inner, outer):
-                bz_arrival(source).wait_recv()
-                bx_copy(source, 1).start()
+            bz_arrival(source).wait_recv()
+            bx_copy(source, 1).start()
 
     def streams_mixed(_):
         with scope("sinkhorn"):
@@ -356,9 +351,9 @@
     def quarter(at):
         return pl.ds(pl.multiple_of(at * gq, gq), gq)
 
-    def c1_copy(job):
-        span = pl.ds(job, BODY)
-        return send(sums.at[span, 1 - core], pair_in.at[span], c1_send.at[0], c1_recv.at[lax.div(job, BODY)], core_peer)
+    def c1_copy(job, size):
+        span = pl.ds(job, size)
+        return send(sums.at[span, 1 - core], pair_in.at[span], c1_send.at[0], c1_recv.at[job], core_peer)
 
     def c2_copy(job, r):
         return send(ring_out.at[job, r - 1], ring_in.at[job, r - 1], c2_send.at[0], c2_recv.at[job], y_peer(r))
@@ -383,11 +378,11 @@
         with scope("far_wait"):
             bx_all(1).wait_recv()
 
-    def c_first(job):
+    def c_first(job, size):
         with scope("c_first"):
             g = job // chunks
             rows = rows_all[pl.ds(g * PAIR * zb, PAIR * zb)].reshape(PAIR * gh, width)
-            for i in range(BODY):
+            for i in range(size):
                 for at, vmem in ((pl.ds(0, nc), gate_v), (pl.ds(nc, nc), up_v)):
                     product = None
                     for kt in range(0, width, nc):
@@ -395,7 +390,7 @@
                         term = jnp.dot(rows[:, kt : kt + nc], block, preferred_element_type=jnp.float32)
                         product = term if product is None else product + term
                     sums[job + i, :, :, at] = product.reshape(PAIR, gh, nc)
-            c1_copy(job).start()
+            c1_copy(job, size).start()
 
     def c_second(job):
         with scope("c_second"):
@@ -489,45 +484,45 @@
                 value = mixed[i, :, cols(n)] + column(post[i], 0) * mlp_out
                 out_ref[i, :, cols(n)] = value.astype(jnp.bfloat16)
 
-    def sum_triple(job):
+    forward(inner)
+    streams_mixed(0)
+    forward(outer)
+    with scope("b_wait"):
+        bz_arrival(mate).wait_recv()
+        bx_all(0).wait_recv()
+
+    def sum_body(job, size):
         with scope("c1_wait"):
-            c1_copy(job).wait_recv()
-        run(c_second, job, BODY)
-
-    def near_ready(_):
+            c1_copy(job, size).wait_recv()
+        run(c_second, job, size)
+
+    lead = [1, BODY - 1] + [BODY] * (chunks // BODY - 1)
+    even = [BODY] * (chunks // BODY)
+    base = chunks / BODY + FAR_GAP
+    timed = [(base - 0.01, far_wait, (0,))]
+    for g, (origin, sizes) in enumerate(((0, lead), (base, even))):
+        done = 0
+        for size in sizes:
+            job = g * chunks + done
+            begin, done = origin + done / BODY, done + size
+            end = origin + done / BODY
+            timed += [
+                (begin, c_first, (job, size)),
+                (end + SUM_AT[g], sum_body, (job, size)),
+                (end + HIDDEN_AT if g else base + NEAR_HIDDEN + begin / LANES, run, (c_third, job, size)),
+                (end + FORWARD_AT if g else base + NEAR_FORWARD + begin / LANES, run, (c_fourth, job, size)),
+            ]
+    for _, stage, values in sorted(timed, key=lambda item: item[0]):
+        stage(*values)
+
+    weight_wait(2)
+    for g in (1, 0):
         with scope("c4_wait"):
-            c4_arrival(0).wait_recv()
-            weight_wait(2)
-
-    triples = chunks // BODY
-    base = triples + FAR_GAP
-    timed = [(0.5, forward, 0), (triples + 0.2, streams_mixed, 0), (base - 0.01, far_wait, 0)]
-    for g, origin in enumerate((0, base)):
-        for i in range(triples):
-            job = g * chunks + i * BODY
-            timed += [
-                (origin + i, c_first, job),
-                (origin + i + SUM_AT, sum_triple, job),
-                (origin + i + HIDDEN_AT, functools.partial(run, c_third, count=BODY), job),
-                (origin + i + FORWARD_AT, functools.partial(run, c_fourth, count=BODY), job),
-            ]
-    for i, (n, count_of) in enumerate(parts):
-        at = NEAR_DOWN[min(i, len(NEAR_DOWN) - 1)]
-        if i == 0:
-            timed.append((at - 0.01, near_ready, 0))
-        timed.append((at, lambda _, n=n, count_of=count_of: d_first(0, n, count_of), 0))
-    for _, stage, job in sorted(timed, key=lambda item: item[0]):
-        if isinstance(stage, functools.partial):
-            stage(first=job)
-        else:
-            stage(job)
-
-    with scope("c4_wait"):
-        c4_arrival(1).wait_recv()
-    for n, count_of in parts:
-        d_first(1, n, count_of)
+            c4_arrival(g).wait_recv()
+        for n, count_of in parts:
+            d_first(g, n, count_of)
+    run(d_far, 0, columns)
     run(d_near, 0, columns)
-    run(d_far, 0, columns)
     run(d_third, 0, columns)
 
     with scope("drain"):
@@ -582,7 +577,7 @@
         ((columns, tok, cc), bf16),
     ]
     sems = [(2,), (3,)]
-    for count in (1, zs, GROUPS, chunks * GROUPS // BODY, chunks * GROUPS, chunks * GROUPS * (ys - 1), GROUPS, jobs, columns):
+    for count in (1, zs, GROUPS, chunks * GROUPS, chunks * GROUPS, chunks * GROUPS * (ys - 1), GROUPS, jobs, columns):
         sems += [(1,), (count,)]
     size = sum(math.prod(shape) * jnp.dtype(kind).itemsize for shape, kind in arrays)
     return arrays, sems, size

time: 43.9 us -> 43.2 us (0.984)
  Pallas kernels: 42.9 us -> 42.2 us
    pallas_call x1, Pallas kernels: 42.9 us -> 42.2 us  [fused(): pl.pallas_call(functools.partial(layer_kernel, plan), out_shape=pltpu.VME...]
where the time goes in v5:
time: 43.2 us; the launch traced here: 43.1 us
  Pallas kernels  42.2 us (98%)
  local copies, waits for them, and re-layouts  0.81 us (2%)
    pallas_call x1, Pallas kernels, fused(): pl.pallas_call(functools.partial(layer_kernel, plan), out_shape=pltpu.VME...  42.2 us

profile of v5, /device:TPU:0, one launch (start us, length us, event | category | flops | bytes accessed | tf_op | source)
XLA Modules:
  0.0 43.1 jit_solution(1527358713788452401)
XLA Ops:
  0.0 42.2 %shard_map.64 = bf16[4,16,1792]{2,1,0:T(8,128)(2,1)S(1)} custom-call(bf16[16,4,1792]{2,1,0:T(4,128)(2,1)} %s_hbm.1, bf16[24,4,1792]{2,1,0:T(4,128)(2,1)} %mw_hbm.1, f32[1,24]{1,0:T(1,128)} %bitcast.3, bf16[2304,1792]{1,0:T(8,128)(2,1)} %gate_hbm.1, bf16[2304,1792]{1,0:T(8,128)(2,1)} %up_hbm.1, bf16[2304,1792]{1,0:T(8,128)(2,1)} %down_hbm.1), custom_call_target="tpu_custom_call" | custom-call | tf_op jit(solution)/shard_map/pallas_call | solution.py:597
  42.2 0.8 %copy.7 = bf16[16,4,1792]{2,1,0:T(4,128)(2,1)} copy(bf16[16,4,1792]{2,0,1:T(8,128)(2,1)S(1)} %bitcast.2) | data formatting | bytes 458752 | tf_op jit(solution)/shard_map/transpose | solution.py:608
